TPU v7x, 512 devices: a whole 4x8x8 slice. The times are simulated.
512 devices in a mesh: gx: 32 (over z, x_hi, core), gy: 16 (over y, x_lo).
Axes of the slice: x: 4 (x_hi: 2, x_lo: 2; x = x_hi * 2 + x_lo), y: 8, z: 8, core: 2. Of those that a mesh axis runs over, the one named last changes fastest.
Arguments:
- init_re: float32 [1, 1024, 16384], P(None, 'gx', 'gy'), may hold values from -6 to 6
- init_im: float32 [1, 1024, 16384], P(None, 'gx', 'gy'), may hold values from -6 to 6
- onsite: float32 [1024, 16384], P('gx', 'gy'), may hold values from -0.9 to 0.9
- bond_x: int32 [1024, 16384], P('gx', 'gy'), may hold values from 0 to 15
- bond_y: int32 [1024, 16384], P('gx', 'gy'), may hold values from 0 to 15
- hop_table: float32 [16], replicated, may hold values from 1.4 to 1.6
- centre: int32 [1, 2], replicated, may hold values from 0 to 1023
- duration: float32 [1], replicated, may hold values from 0.55 to 0.6
Outputs:
- out_re: float32 [1, 1024, 16384], P(None, 'gx', 'gy')
- out_im: float32 [1, 1024, 16384], P(None, 'gx', 'gy')
- term_norms: float32 [2, 8, 1], replicated
All inputs are finite; a program needn't handle non-finite values.
Results may differ from a plain program's by a relative error of at most 0.0003.
Values sent between devices are 32-bit elements; how exact they have to be, the bound alone decides.
No kernel may reach another device: no remote copies, remote signals or barrier semaphores. Data moves between devices by JAX's collectives and lax.ppermute only.
A program may use at most 64 MiB of HBM per device.

v0:
```python
import math

import jax
import jax.numpy as jnp
from jax import lax
from jax.sharding import Mesh
from jax.sharding import PartitionSpec as P

TERMS = 8
STEPS = 2
GX = ("gx_0", "gx_1", "gx_2")
GY = ("gy_0", "gy_1")
GX_GY = ("gx_0", "gx_1", "gx_2", "gy_0", "gy_1")


SPECTRAL = 7.5
epsilon = 1e-06


def padded(block, sides, width):
    for axis, dim in sides:
        count = lax.axis_size(axis)
        forward = [(i, i + 1) for i in range(count - 1)]
        forward.append((count - 1, 0))
        backward = [(target, source) for source, target in forward]
        low = lax.ppermute(
            lax.slice_in_dim(block, block.shape[dim] - width, None, axis=dim), axis, forward
        )
        high = lax.ppermute(lax.slice_in_dim(block, 0, width, axis=dim), axis, backward)
        block = jnp.concatenate([low, block, high], axis=dim)
    return block


def over_axes(value, axes):
    for axis in axes:
        value = lax.psum(value, axis)
    return value


def bessel_weights(duration):
    argument = duration[0] * SPECTRAL
    halved = argument * 0.5
    weights = []
    for degree in range(TERMS):
        series = halved**degree / math.factorial(degree)
        summed = series
        for counter in range(1, 24):
            series = series * -(halved * halved) / (counter * (counter + degree))
            summed = summed + series
        weights.append(summed if degree == 0 else 2.0 * summed)
    return weights


def rotated(degree, real_part, imag_part):
    quarter = degree % 4
    if quarter == 0:
        return (real_part, imag_part)
    if quarter == 1:
        return (imag_part, -real_part)
    if quarter == 2:
        return (-real_part, -imag_part)
    return (-imag_part, real_part)


def falloff(positions, centres, extent):
    distance = jnp.mod(positions[None, :] - centres[:, None], extent)
    distance = jnp.minimum(distance, extent - distance).astype(jnp.float32)
    return distance * distance * (4.5 / (extent * extent))


def shrink(tensor, margin):
    if margin == 0:
        return tensor
    return tensor[..., margin : tensor.shape[-2] - margin, margin : tensor.shape[-1] - margin]


def apply_wide(grid_field, coeffs):
    potential = coeffs[0]
    hop_rows = coeffs[1]
    hop_cols = coeffs[2]
    result = potential[1:-1, 1:-1] * grid_field[..., 1:-1, 1:-1]
    result = result - hop_rows[1:-1, 1:-1] * grid_field[..., 2:, 1:-1]
    result = result - hop_rows[:-2, 1:-1] * grid_field[..., :-2, 1:-1]
    result = result - hop_cols[1:-1, 1:-1] * grid_field[..., 1:-1, 2:]
    result = result - hop_cols[1:-1, :-2] * grid_field[..., 1:-1, :-2]
    return result * (1.0 / SPECTRAL)


def per_device(init_re, init_im, onsite, bond_x, bond_y, hop_table, centre, duration):
    packets, rows_local, cols_local = init_re.shape
    rows_total = rows_local * lax.axis_size(GX)
    cols_total = cols_local * lax.axis_size(GY)
    cell_count = rows_total * cols_total
    classes = hop_table.shape[0]
    selector = jnp.arange(classes, dtype=jnp.int32)[:, None, None]
    table_column = hop_table[:, None, None]
    hop_down = jnp.sum(jnp.where(bond_x[None] == selector, table_column, 0.0), axis=0)
    hop_right = jnp.sum(jnp.where(bond_y[None] == selector, table_column, 0.0), axis=0)
    weights = bessel_weights(duration)
    row_index = lax.axis_index(GX) * rows_local + lax.iota(jnp.int32, rows_local)
    col_index = lax.axis_index(GY) * cols_local + lax.iota(jnp.int32, cols_local)
    row_fall = falloff(row_index, centre[:, 0], rows_total)
    col_fall = falloff(col_index, centre[:, 1], cols_total)
    envelope = jnp.exp(-(row_fall[:, :, None] + col_fall[:, None, :]))
    packet_state = jnp.stack([init_re * envelope, init_im * envelope])
    reach = TERMS - 1
    coeffs = padded(jnp.stack([onsite, hop_down, hop_right]), ((GX, 1), (GY, 2)), reach)
    norm_rows = []
    local_terms = []
    local_states = []
    for repeat in range(STEPS):
        current = padded(packet_state, ((GX, 2), (GY, 3)), reach)
        margin = reach
        previous = current
        previous_margin = reach
        chebyshev = [packet_state]
        for chebyshev_degree in range(1, TERMS):
            applied = apply_wide(current, shrink(coeffs, reach - margin))
            if chebyshev_degree == 1:
                following = applied
            else:
                following = 2.0 * applied - shrink(previous, previous_margin - margin + 1)
            previous, previous_margin = (current, margin)
            current = following
            margin = margin - 1
            chebyshev.append(shrink(following, margin))
        accumulate = weights[0] * packet_state
        for degree in range(1, TERMS):
            real_rot, imag_rot = rotated(degree, chebyshev[degree][0], chebyshev[degree][1])
            accumulate = accumulate + weights[degree] * jnp.stack([real_rot, imag_rot])
        term_local = jnp.stack([jnp.sum(vector * vector, axis=(0, 2, 3)) for vector in chebyshev])
        state_local = jnp.sum(accumulate * accumulate, axis=(0, 2, 3))
        local_terms.append(term_local)
        local_states.append(state_local)
        packet_state = accumulate
    term_totals, state_totals = (
        over_axes(jnp.stack(local_terms), GX_GY),
        over_axes(jnp.stack(local_states), GX_GY),
    )
    factor = jnp.ones((packets,), jnp.float32)
    for repeat in range(STEPS):
        squared = factor * factor
        norm_rows.append(term_totals[repeat] / cell_count * squared)
        true_mean = state_totals[repeat] / cell_count * squared
        factor = factor * lax.rsqrt(true_mean + epsilon)
    packet_state = packet_state * factor[None, :, None, None]
    return (packet_state[0], packet_state[1], jnp.stack(norm_rows))


def solution(mesh):
    finer = Mesh(mesh.devices.reshape(8, 2, 2, 8, 2), ("gx_0", "gx_1", "gx_2", "gy_0", "gy_1"))
    in_specs = (P(None, GX, GY), P(None, GX, GY), P(GX, GY), P(GX, GY), P(GX, GY), P(), P(), P())
    out_specs = (P(None, GX, GY), P(None, GX, GY), P())
    return jax.shard_map(
        per_device, mesh=finer, in_specs=in_specs, out_specs=out_specs, check_vma=False
    )
```

profile of v0, /device:TPU:2, one launch (start us, length us, event | category | flops | bytes accessed | tf_op | source)
XLA Modules:
  0.0 154.3 jit_solution(2345416832036996871)
XLA Ops:
  0.7 1.3 fusion.129
  2.0 0.7 fusion.100
  2.6 0.7 fusion.97
  3.3 1.1 multiply_bitcast_fusion
  4.4 1.9 %collective-permute-start.4 = (f32[2,1,7,1024]{3,2,1,0:T(8,128)S(1)}, f32[2,1,7,1024]{3,2,1,0:T(8,128)S(1)}, u32[]{:S(2)}, u32[]{:S(2)}) collective-permute-start(f32[2,1,7,1024]{3,2,1,0:T(8,128)S(1)} %get-tuple-element.84), channel_id=1, source_target_pairs={{0,16},{16,32},{32,48},{48,64},{64,80},{80,96},{96,112},{112,128},... | collective-permute-start | bytes 172040 | tf_op jit(solution)/shard_map/ppermute | solution.py:26
  6.4 11.9 %collective-permute-start.5 = (f32[2,1,7,1024]{3,2,1,0:T(8,128)S(1)}, f32[2,1,7,1024]{3,2,1,0:T(8,128)S(1)}, u32[]{:S(2)}, u32[]{:S(2)}) collective-permute-start(f32[2,1,7,1024]{3,2,1,0:T(8,128)S(1)} %get-tuple-element.85), channel_id=1, source_target_pairs={{16,0},{32,16},{48,32},{64,48},{80,64},{96,80},{112,96},{128,112},... | collective-permute-start | bytes 172040 | tf_op jit(solution)/shard_map/ppermute | solution.py:29
  18.4 0.5 select_reduce_fusion.1
  18.9 1.9 %collective-permute-start = (f32[3,7,1024]{2,1,0:T(8,128)S(1)}, f32[3,7,1024]{2,1,0:T(8,128)S(1)}, u32[]{:S(2)}, u32[]{:S(2)}) collective-permute-start(f32[3,7,1024]{2,1,0:T(8,128)S(1)} %get-tuple-element.56), channel_id=1, source_target_pairs={{0,16},{16,32},{32,48},{48,64},{64,80},{80,96},{96,112},{112,128},... | collective-permute-start | bytes 258056 | tf_op jit(solution)/shard_map/ppermute | solution.py:26
  20.8 7.3 %collective-permute-start.1 = (f32[3,7,1024]{2,1,0:T(8,128)S(1)}, f32[3,7,1024]{2,1,0:T(8,128)S(1)}, u32[]{:S(2)}, u32[]{:S(2)}) collective-permute-start(f32[3,7,1024]{2,1,0:T(8,128)S(1)} %get-tuple-element.57), channel_id=1, source_target_pairs={{16,0},{32,16},{48,32},{64,48},{80,64},{96,80},{112,96},{128,112},... | collective-permute-start | bytes 258056 | tf_op jit(solution)/shard_map/ppermute | solution.py:29
  29.4 0.6 multiply_reduce_fusion.8
  30.4 3.3 %collective-permute-start.3 = (f32[3,46,7]{2,1,0:T(8,128)S(1)}, f32[3,46,7]{2,1,0:T(8,128)S(1)}, u32[]{:S(2)}, u32[]{:S(2)}) collective-permute-start(f32[3,46,7]{2,1,0:T(8,128)S(1)} %get-tuple-element.44), channel_id=1, source_target_pairs={{1,0},{2,1},{3,2},{4,3},{5,4},{6,5},{7,6},{8,7},{9,8},{10,9},{11,1... | collective-permute-start | bytes 11600 | tf_op jit(solution)/shard_map/ppermute | solution.py:29
  33.8 3.4 %collective-permute-start.2 = (f32[3,46,7]{2,1,0:T(8,128)S(1)}, f32[3,46,7]{2,1,0:T(8,128)S(1)}, u32[]{:S(2)}, u32[]{:S(2)}) collective-permute-start(f32[3,46,7]{2,1,0:T(8,128)S(1)} %get-tuple-element.45), channel_id=1, source_target_pairs={{0,1},{1,2},{2,3},{3,4},{4,5},{5,6},{6,7},{7,8},{8,9},{9,10},{10,1... | collective-permute-start | bytes 11600 | tf_op jit(solution)/shard_map/ppermute | solution.py:26
  37.3 3.9 %collective-permute-start.7 = (f32[2,1,46,7]{3,2,1,0:T(8,128)S(1)}, f32[2,1,46,7]{3,2,1,0:T(8,128)S(1)}, u32[]{:S(2)}, u32[]{:S(2)}) collective-permute-start(f32[2,1,46,7]{3,2,1,0:T(8,128)S(1)} %get-tuple-element.58), channel_id=1, source_target_pairs={{1,0},{2,1},{3,2},{4,3},{5,4},{6,5},{7,6},{8,7},{9,8},{10,9},{11,1... | collective-permute-start | bytes 7736 | tf_op jit(solution)/shard_map/ppermute | solution.py:29
  41.2 2.8 %collective-permute-start.6 = (f32[2,1,46,7]{3,2,1,0:T(8,128)S(1)}, f32[2,1,46,7]{3,2,1,0:T(8,128)S(1)}, u32[]{:S(2)}, u32[]{:S(2)}) collective-permute-start(f32[2,1,46,7]{3,2,1,0:T(8,128)S(1)} %get-tuple-element.59), channel_id=1, source_target_pairs={{0,1},{1,2},{2,3},{3,4},{4,5},{5,6},{6,7},{7,8},{8,9},{9,10},{10,1... | collective-permute-start | bytes 7736 | tf_op jit(solution)/shard_map/ppermute | solution.py:26
  44.1 5.1 %collective-permute-done.6 = f32[2,1,46,7]{3,2,1,0:T(8,128)S(1)} collective-permute-done((f32[2,1,46,7]{3,2,1,0:T(8,128)S(1)}, f32[2,1,46,7]{3,2,1,0:T(8,128)S(1)}, u32[]{:S(2)}, u32[]{:S(2)}) %collective-permute-start.6) | collective-permute-done | bytes 2608 | tf_op jit(solution)/shard_map/ppermute | solution.py:26
  49.5 0.4 concatenate.131
  50.8 0.2 slice_bitcast_fusion.2
  51.0 0.2 slice_bitcast_fusion.5
  51.4 0.2 fusion.118
  51.7 0.5 fusion.16
  52.2 0.8 fusion.65
  53.3 0.2 fusion.116
  53.5 0.7 slice_subtract_fusion.1
  54.2 0.8 fusion.64
  56.0 0.4 copy-done.6
  56.4 0.6 slice_subtract_fusion.9
  57.7 0.6 slice_subtract_fusion.8
  58.5 0.6 slice_subtract_fusion.7
  59.5 0.6 slice_subtract_fusion.6
  60.7 1.1 multiply_reduce_fusion.4
  61.8 0.9 multiply_reduce_fusion.10
  62.8 1.9 %collective-permute-start.8 = (f32[2,1,7,1024]{3,2,1,0:T(8,128)S(1)}, f32[2,1,7,1024]{3,2,1,0:T(8,128)S(1)}, u32[]{:S(2)}, u32[]{:S(2)}) collective-permute-start(f32[2,1,7,1024]{3,2,1,0:T(8,128)S(1)} %get-tuple-element.80), channel_id=1, source_target_pairs={{0,16},{16,32},{32,48},{48,64},{64,80},{80,96},{96,112},{112,128},... | collective-permute-start | bytes 172040 | tf_op jit(solution)/shard_map/ppermute | solution.py:26
  64.7 7.3 %collective-permute-start.9 = (f32[2,1,7,1024]{3,2,1,0:T(8,128)S(1)}, f32[2,1,7,1024]{3,2,1,0:T(8,128)S(1)}, u32[]{:S(2)}, u32[]{:S(2)}) collective-permute-start(f32[2,1,7,1024]{3,2,1,0:T(8,128)S(1)} %get-tuple-element.81), channel_id=1, source_target_pairs={{16,0},{32,16},{48,32},{64,48},{80,64},{96,80},{112,96},{128,112},... | collective-permute-start | bytes 172040 | tf_op jit(solution)/shard_map/ppermute | solution.py:29
  72.0 0.8 fusion.63
  72.8 1.1 collective-permute-done.9
  74.0 6.0 %collective-permute-start.11 = (f32[2,1,46,7]{3,2,1,0:T(8,128)S(1)}, f32[2,1,46,7]{3,2,1,0:T(8,128)S(1)}, u32[]{:S(2)}, u32[]{:S(2)}) collective-permute-start(f32[2,1,46,7]{3,2,1,0:T(8,128)S(1)} %get-tuple-element.54), channel_id=1, source_target_pairs={{1,0},{2,1},{3,2},{4,3},{5,4},{6,5},{7,6},{8,7},{9,8},{10,9},{11,1... | collective-permute-start | bytes 7736 | tf_op jit(solution)/shard_map/ppermute | solution.py:29
  80.0 2.1 %collective-permute-start.10 = (f32[2,1,46,7]{3,2,1,0:T(8,128)S(1)}, f32[2,1,46,7]{3,2,1,0:T(8,128)S(1)}, u32[]{:S(2)}, u32[]{:S(2)}) collective-permute-start(f32[2,1,46,7]{3,2,1,0:T(8,128)S(1)} %get-tuple-element.55), channel_id=1, source_target_pairs={{0,1},{1,2},{2,3},{3,4},{4,5},{5,6},{6,7},{7,8},{8,9},{9,10},{10,1... | collective-permute-start | bytes 7736 | tf_op jit(solution)/shard_map/ppermute | solution.py:26
  82.2 0.8 multiply_reduce_fusion.7
  82.9 5.1 %stack.186 = f32[8,1]{0,1:T(1,128)S(1)} concatenate(f32[1,1]{0,1:T(1,128)} %bitcast.36, f32[1,1]{0,1:T(1,128)} %bitcast.37, f32[1,1]{0,1:T(1,128)} %bitcast.38, f32[1,1]{0,1:T(1,128)} %bitcast.39, f32[1,1]{0,1:T(1,128)} %bitcast.40, f32[1,1]{0,1:T(1,128)} %bitcast.41, f32[1,1]{0,1:T(1,128)} %bitcast.42, f32[1,1]{0,1:T(1,128)} %bitcast.43), dimensions={0} | concatenate | bytes 64 | tf_op jit(solution)/shard_map/stack | solution.py:131
  88.0 0.3 concatenate.135
  88.3 0.5 fusion.6
  88.8 0.7 fusion.62
  89.6 0.7 slice_subtract_fusion
  90.2 0.8 fusion.61
  91.1 0.6 slice_subtract_fusion.5
  91.7 0.7 fusion.60
  92.5 0.6 slice_subtract_fusion.4
  93.0 0.8 multiply_reduce_fusion.3
  93.8 0.6 slice_subtract_fusion.3
  94.7 0.6 copy-done.25
  95.6 0.6 slice_subtract_fusion.2
  96.2 0.3 copy-done.41
  96.8 1.0 multiply_reduce_fusion
  98.2 5.1 %stack.195 = f32[8,1]{0,1:T(1,128)S(1)} concatenate(f32[1,1]{0,1:T(1,128)} %bitcast.29, f32[1,1]{0,1:T(1,128)} %bitcast.45, f32[1,1]{0,1:T(1,128)} %bitcast.46, f32[1,1]{0,1:T(1,128)} %bitcast.47, f32[1,1]{0,1:T(1,128)} %bitcast.48, f32[1,1]{0,1:T(1,128)} %bitcast.49, f32[1,1]{0,1:T(1,128)} %bitcast.50, f32[1,1]{0,1:T(1,128)} %bitcast.51), dimensions={0} | concatenate | bytes 64 | tf_op jit(solution)/shard_map/stack | solution.py:131
  103.4 0.8 multiply_reduce_fusion.9
  104.2 1.4 pad_maximum_fusion.9
  105.6 14.8 %all-reduce.1 = (f32[2,1]{0,1:T(1,128)S(1)}, f32[2,8,1]{1,2,0:T(1,128)S(1)}) all-reduce(f32[2,1]{0,1:T(1,128)S(1)} %pad_maximum_fusion.9, f32[2,8,1]{1,2,0:T(1,128)S(1)} %pad_maximum_fusion.7), channel_id=1, replica_groups=mesh['gx_0'=8,'gx_1'=2,'gx_2'=2,'gy_0'=8,'gy_1'=2] {'gx_0'}, use_global_device_ids=true, to_apply=%region_4.5 | all-reduce | flops 18 | bytes 144 | tf_op jit(solution)/shard_map/psum | solution.py:36
  120.5 6.4 %all-reduce.4 = (f32[2,1]{0,1:T(1,128)S(1)}, f32[2,8,1]{1,2,0:T(1,128)S(1)}) all-reduce(f32[2,1]{0,1:T(1,128)S(1)} %get-tuple-element.7, f32[2,8,1]{1,2,0:T(1,128)S(1)} %get-tuple-element.8), channel_id=1, replica_groups=mesh['gx_0'=8,'gx_1'=2,'gx_2'=2,'gy_0'=8,'gy_1'=2] {'gx_1'}, use_global_device_ids=true, to_apply=%region_5.6 | all-reduce | flops 18 | bytes 144 | tf_op jit(solution)/shard_map/psum | solution.py:36
  126.9 2.4 %all-reduce.3 = (f32[2,1]{0,1:T(1,128)S(1)}, f32[2,8,1]{1,2,0:T(1,128)S(1)}) all-reduce(f32[2,1]{0,1:T(1,128)S(1)} %get-tuple-element.13, f32[2,8,1]{1,2,0:T(1,128)S(1)} %get-tuple-element.14), channel_id=1, replica_groups=mesh['gx_0'=8,'gx_1'=2,'gx_2'=2,'gy_0'=8,'gy_1'=2] {'gx_2'}, use_global_device_ids=true, to_apply=%region_6.7 | all-reduce | flops 18 | bytes 144 | tf_op jit(solution)/shard_map/psum | solution.py:36
  129.3 16.8 %all-reduce = (f32[2,1]{0,1:T(1,128)S(1)}, f32[2,8,1]{1,2,0:T(1,128)S(1)}) all-reduce(f32[2,1]{0,1:T(1,128)S(1)} %get-tuple-element.11, f32[2,8,1]{1,2,0:T(1,128)S(1)} %get-tuple-element.12), channel_id=1, replica_groups=mesh['gx_0'=8,'gx_1'=2,'gx_2'=2,'gy_0'=8,'gy_1'=2] {'gy_0'}, use_global_device_ids=true, to_apply=%region_7.8 | all-reduce | flops 18 | bytes 144 | tf_op jit(solution)/shard_map/psum | solution.py:36
  146.1 4.9 %all-reduce.2 = (f32[2,1]{0,1:T(1,128)S(1)}, f32[2,8,1]{1,2,0:T(1,128)S(1)}) all-reduce(f32[2,1]{0,1:T(1,128)S(1)} %get-tuple-element.5, f32[2,8,1]{1,2,0:T(1,128)S(1)} %get-tuple-element.6), channel_id=1, replica_groups=mesh['gx_0'=8,'gx_1'=2,'gx_2'=2,'gy_0'=8,'gy_1'=2] {'gy_1'}, use_global_device_ids=true, to_apply=%region_8.9 | all-reduce | flops 18 | bytes 144 | tf_op jit(solution)/shard_map/psum | solution.py:36
  151.0 0.6 fusion.128
  153.0 0.7 slice_bitcast_fusion.21
  153.8 0.6 pad_maximum_fusion.8
  (157 shorter events, 6.3 us)
Async XLA Ops:
  0.6 17.7 %copy-start.53 = (f32[16]{0:T(128)S(1)}, f32[16]{0:T(128)}, u32[]{:S(2)}) copy-start(f32[16]{0:T(128)} %param.13) | copy-start | bytes 196
  0.6 17.7 %copy-start.52 = (s32[32,1024]{1,0:T(8,128)S(1)}, s32[32,1024]{1,0:T(8,128)}, u32[]{:S(2)}) copy-start(s32[32,1024]{1,0:T(8,128)} %param.12) | copy-start | bytes 393220
  0.7 17.7 %copy-start.51 = (s32[32,1024]{1,0:T(8,128)S(1)}, s32[32,1024]{1,0:T(8,128)}, u32[]{:S(2)}) copy-start(s32[32,1024]{1,0:T(8,128)} %param.11) | copy-start | bytes 393220
  3.3 15.5 %copy-start.50 = (f32[32,1024]{1,0:T(8,128)S(1)}, f32[32,1024]{1,0:T(8,128)}, u32[]{:S(2)}) copy-start(f32[32,1024]{1,0:T(8,128)} %param.10) | copy-start | bytes 393220
  4.4 25.6 %collective-permute-start.4 = (f32[2,1,7,1024]{3,2,1,0:T(8,128)S(1)}, f32[2,1,7,1024]{3,2,1,0:T(8,128)S(1)}, u32[]{:S(2)}, u32[]{:S(2)}) collective-permute-start(f32[2,1,7,1024]{3,2,1,0:T(8,128)S(1)} %get-tuple-element.84), channel_id=1, source_target_pairs={{0,16},{16,32},{32,48},{48,64},{64,80},{80,96},{96,112},{112,128},... | collective-permute-start | bytes 172040 | tf_op jit(solution)/shard_map/ppermute | solution.py:26
  6.4 23.6 %collective-permute-start.5 = (f32[2,1,7,1024]{3,2,1,0:T(8,128)S(1)}, f32[2,1,7,1024]{3,2,1,0:T(8,128)S(1)}, u32[]{:S(2)}, u32[]{:S(2)}) collective-permute-start(f32[2,1,7,1024]{3,2,1,0:T(8,128)S(1)} %get-tuple-element.85), channel_id=1, source_target_pairs={{16,0},{32,16},{48,32},{64,48},{80,64},{96,80},{112,96},{128,112},... | collective-permute-start | bytes 172040 | tf_op jit(solution)/shard_map/ppermute | solution.py:29
  18.9 11.2 %collective-permute-start = (f32[3,7,1024]{2,1,0:T(8,128)S(1)}, f32[3,7,1024]{2,1,0:T(8,128)S(1)}, u32[]{:S(2)}, u32[]{:S(2)}) collective-permute-start(f32[3,7,1024]{2,1,0:T(8,128)S(1)} %get-tuple-element.56), channel_id=1, source_target_pairs={{0,16},{16,32},{32,48},{48,64},{64,80},{80,96},{96,112},{112,128},... | collective-permute-start | bytes 258056 | tf_op jit(solution)/shard_map/ppermute | solution.py:26
  20.8 9.5 %collective-permute-start.1 = (f32[3,7,1024]{2,1,0:T(8,128)S(1)}, f32[3,7,1024]{2,1,0:T(8,128)S(1)}, u32[]{:S(2)}, u32[]{:S(2)}) collective-permute-start(f32[3,7,1024]{2,1,0:T(8,128)S(1)} %get-tuple-element.57), channel_id=1, source_target_pairs={{16,0},{32,16},{48,32},{64,48},{80,64},{96,80},{112,96},{128,112},... | collective-permute-start | bytes 258056 | tf_op jit(solution)/shard_map/ppermute | solution.py:29
  30.4 19.1 %collective-permute-start.3 = (f32[3,46,7]{2,1,0:T(8,128)S(1)}, f32[3,46,7]{2,1,0:T(8,128)S(1)}, u32[]{:S(2)}, u32[]{:S(2)}) collective-permute-start(f32[3,46,7]{2,1,0:T(8,128)S(1)} %get-tuple-element.44), channel_id=1, source_target_pairs={{1,0},{2,1},{3,2},{4,3},{5,4},{6,5},{7,6},{8,7},{9,8},{10,9},{11,1... | collective-permute-start | bytes 11600 | tf_op jit(solution)/shard_map/ppermute | solution.py:29
  33.8 15.8 %collective-permute-start.2 = (f32[3,46,7]{2,1,0:T(8,128)S(1)}, f32[3,46,7]{2,1,0:T(8,128)S(1)}, u32[]{:S(2)}, u32[]{:S(2)}) collective-permute-start(f32[3,46,7]{2,1,0:T(8,128)S(1)} %get-tuple-element.45), channel_id=1, source_target_pairs={{0,1},{1,2},{2,3},{3,4},{4,5},{5,6},{6,7},{7,8},{8,9},{9,10},{10,1... | collective-permute-start | bytes 11600 | tf_op jit(solution)/shard_map/ppermute | solution.py:26
  37.3 6.9 %collective-permute-start.7 = (f32[2,1,46,7]{3,2,1,0:T(8,128)S(1)}, f32[2,1,46,7]{3,2,1,0:T(8,128)S(1)}, u32[]{:S(2)}, u32[]{:S(2)}) collective-permute-start(f32[2,1,46,7]{3,2,1,0:T(8,128)S(1)} %get-tuple-element.58), channel_id=1, source_target_pairs={{1,0},{2,1},{3,2},{4,3},{5,4},{6,5},{7,6},{8,7},{9,8},{10,9},{11,1... | collective-permute-start | bytes 7736 | tf_op jit(solution)/shard_map/ppermute | solution.py:29
  41.2 8.1 %collective-permute-start.6 = (f32[2,1,46,7]{3,2,1,0:T(8,128)S(1)}, f32[2,1,46,7]{3,2,1,0:T(8,128)S(1)}, u32[]{:S(2)}, u32[]{:S(2)}) collective-permute-start(f32[2,1,46,7]{3,2,1,0:T(8,128)S(1)} %get-tuple-element.59), channel_id=1, source_target_pairs={{0,1},{1,2},{2,3},{3,4},{4,5},{5,6},{6,7},{7,8},{8,9},{9,10},{10,1... | collective-permute-start | bytes 7736 | tf_op jit(solution)/shard_map/ppermute | solution.py:26
  53.5 0.7 copy-start
  55.4 2.3 %copy-start.4 = (f32[38,1030]{1,0:T(8,128)}, f32[38,1030]{1,0:T(8,128)S(1)}, u32[]{:S(2)}) copy-start(f32[38,1030]{1,0:T(8,128)S(1)} %slice.930) | copy-start | bytes 469684
  55.5 3.0 %copy-start.2 = (f32[36,1028]{1,0:T(8,128)}, f32[36,1028]{1,0:T(8,128)S(1)}, u32[]{:S(2)}) copy-start(f32[36,1028]{1,0:T(8,128)S(1)} %slice.944) | copy-start | bytes 444100
  55.6 5.1 %copy-start.40 = (f32[32,1024]{1,0:T(8,128)}, f32[32,1024]{1,0:T(8,128)S(1)}, u32[]{:S(2)}) copy-start(f32[32,1024]{1,0:T(8,128)S(1)} %slice.976) | copy-start | bytes 393220
  56.0 1.0 copy-start.8
  56.0 1.0 copy-start.10
  56.0 1.0 copy-start.12
  56.0 1.0 copy-start.14
  57.4 1.2 copy-start.16
  57.4 1.2 copy-start.18
  57.4 1.1 copy-start.20
  57.4 1.1 copy-start.22
  57.6 0.7 copy-start.32
  57.6 0.8 copy-start.34
  57.6 0.8 copy-start.36
  57.6 0.9 copy-start.38
  59.5 0.7 copy-start.26
  59.5 0.8 copy-start.28
  59.5 0.8 copy-start.30
  60.6 1.2 copy-start.42
  60.7 1.1 copy-start.44
  60.7 1.1 copy-start.46
  60.7 1.1 copy-start.48
  62.8 10.0 %collective-permute-start.8 = (f32[2,1,7,1024]{3,2,1,0:T(8,128)S(1)}, f32[2,1,7,1024]{3,2,1,0:T(8,128)S(1)}, u32[]{:S(2)}, u32[]{:S(2)}) collective-permute-start(f32[2,1,7,1024]{3,2,1,0:T(8,128)S(1)} %get-tuple-element.80), channel_id=1, source_target_pairs={{0,16},{16,32},{32,48},{48,64},{64,80},{80,96},{96,112},{112,128},... | collective-permute-start | bytes 172040 | tf_op jit(solution)/shard_map/ppermute | solution.py:26
  64.7 9.1 %collective-permute-start.9 = (f32[2,1,7,1024]{3,2,1,0:T(8,128)S(1)}, f32[2,1,7,1024]{3,2,1,0:T(8,128)S(1)}, u32[]{:S(2)}, u32[]{:S(2)}) collective-permute-start(f32[2,1,7,1024]{3,2,1,0:T(8,128)S(1)} %get-tuple-element.81), channel_id=1, source_target_pairs={{16,0},{32,16},{48,32},{64,48},{80,64},{96,80},{112,96},{128,112},... | collective-permute-start | bytes 172040 | tf_op jit(solution)/shard_map/ppermute | solution.py:29
  74.0 14.0 %collective-permute-start.11 = (f32[2,1,46,7]{3,2,1,0:T(8,128)S(1)}, f32[2,1,46,7]{3,2,1,0:T(8,128)S(1)}, u32[]{:S(2)}, u32[]{:S(2)}) collective-permute-start(f32[2,1,46,7]{3,2,1,0:T(8,128)S(1)} %get-tuple-element.54), channel_id=1, source_target_pairs={{1,0},{2,1},{3,2},{4,3},{5,4},{6,5},{7,6},{8,7},{9,8},{10,9},{11,1... | collective-permute-start | bytes 7736 | tf_op jit(solution)/shard_map/ppermute | solution.py:29
  80.0 8.0 %collective-permute-start.10 = (f32[2,1,46,7]{3,2,1,0:T(8,128)S(1)}, f32[2,1,46,7]{3,2,1,0:T(8,128)S(1)}, u32[]{:S(2)}, u32[]{:S(2)}) collective-permute-start(f32[2,1,46,7]{3,2,1,0:T(8,128)S(1)} %get-tuple-element.55), channel_id=1, source_target_pairs={{0,1},{1,2},{2,3},{3,4},{4,5},{5,6},{6,7},{7,8},{8,9},{9,10},{10,1... | collective-permute-start | bytes 7736 | tf_op jit(solution)/shard_map/ppermute | solution.py:26
  88.3 1.3 copy-start.1
  89.6 1.5 copy-start.7
  89.6 1.5 copy-start.9
  89.6 1.5 copy-start.11
  89.6 1.5 copy-start.13
  89.6 1.5 copy-start.15
  91.0 1.4 copy-start.5
  91.0 1.4 copy-start.33
  91.1 1.4 copy-start.35
  91.1 1.3 copy-start.37
  91.1 1.3 copy-start.39
  92.4 1.4 copy-start.3
  92.4 1.4 copy-start.17
  92.4 1.4 copy-start.19
  92.5 1.4 copy-start.21
  92.5 1.4 copy-start.23
  94.4 0.9 copy-start.25
  94.4 1.0 copy-start.27
  94.4 1.1 copy-start.29
  94.4 1.2 copy-start.31
  95.6 0.9 copy-start.41
  95.6 1.0 copy-start.43
  95.6 1.0 copy-start.45
  95.6 1.1 copy-start.47
  95.6 1.2 copy-start.49
  (2 other events, 1.4 us)
where the time goes:
time: 155 us; the launch traced here: 154 us
  starting transfers between devices  53.8 us (35%)
  blocking collectives  45.4 us (29%)
  other arithmetic  23.9 us (15%)
  local copies, waits for them, and re-layouts  20.2 us (13%)
  waiting for transfers between devices  6.46 us (4%)
  between operations  4.46 us (3%)
    psum x5, blocking collectives, over_axes(): value = lax.psum(value, axis)  45.4 us
    ppermute x6, starting transfers between devices, padded(): lax.ppermute(lax.slice_in_dim(block, 0, width, axis=dim), axis, backward)  39.7 us
    ppermute x6, starting transfers between devices, padded(): lax.ppermute(lax.slice_in_dim(block, block.shape[dim] - width, None, axis...  14.1 us
    another operation x2, local copies, waits for them, and re-layouts, per_device(): jnp.stack([jnp.sum(vector * vector, axis=(0, 2, 3)) for vector in chebysh...  10.2 us
    reduce_sum x11, other arithmetic, per_device(): jnp.sum(vector * vector, axis=(0, 2, 3))  8.87 us
    sub x10, other arithmetic, per_device(): following = 2.0 * applied - shrink(previous, previous_margin - margin + 1)  5.76 us
    ppermute x6, waiting for transfers between devices, padded(): lax.ppermute(lax.slice_in_dim(block, block.shape[dim] - width, None, axis...  5.16 us
  transfers between devices with their start and end apart: 12, of which 3 were waited for; matrix products, arithmetic and copies ran while one was open for 5% of the time, Pallas kernels for 0%

commit v1 on v0

v1 whole, which is shorter than its diff:
```python
import functools
import math

import jax
import jax.numpy as jnp
from jax import lax
from jax.experimental import pallas as pl
from jax.experimental.pallas import tpu as pltpu
from jax.sharding import PartitionSpec as P

TERMS = 8
STEPS = 2
SPECTRAL = 7.5
EPSILON = 1e-06
REACH = STEPS * (TERMS - 1)
LANES = 128
GAP = 16
PAD = 8
TOP = 16
FIELDS = 5
VMEM = pltpu.VMEM
SMEM = pltpu.SMEM


def lane_of(shape):
    return lax.broadcasted_iota(jnp.int32, shape, len(shape) - 1)


def falloff(positions, centre, extent):
    distance = positions - centre
    distance = jnp.where(distance < 0, distance + extent, distance)
    distance = jnp.minimum(distance, extent - distance).astype(jnp.float32)
    return jnp.exp(-(distance * distance * (4.5 / (extent * extent))))


def row_envelope(start, count, row_base, centre, extent):
    positions = row_base + start + lax.broadcasted_iota(jnp.int32, (count, LANES), 0)
    return falloff(positions, centre, extent)


def column_envelope(tile, column_base, centre, extent):
    positions = column_base + tile * LANES + lane_of((1, LANES))
    return falloff(positions, centre, extent)


def table_lanes(table_ref, classes):
    lane = lane_of((8, LANES))
    table = jnp.zeros((8, LANES), jnp.float32)
    for entry in range(classes):
        table = jnp.where(lane == entry, table_ref[entry], table)
    return table


def looked_up(table, codes):
    rows = codes.shape[0]
    whole = jnp.concatenate([table] * -(-rows // 8), axis=0)[:rows]
    return jnp.take_along_axis(whole, codes, axis=1)


def bases(rows, cols, gx, gy):
    return lax.axis_index(gx) * rows, lax.axis_index(gy) * cols


def fields_of(refs, table, rows, tile, envelope):
    re_ref, im_ref, onsite_ref, down_ref, right_ref = refs
    cut = (slice(*rows), pl.ds(tile * LANES, LANES))
    return [
        re_ref[0, cut[0], cut[1]] * envelope,
        im_ref[0, cut[0], cut[1]] * envelope,
        onsite_ref[cut],
        looked_up(table, down_ref[cut]),
        looked_up(table, right_ref[cut]),
    ]


def strip_kernel(gx, gy, extents, table_ref, centre_ref, re, im, onsite, down, right, west_ref, east_ref):
    rows, cols = onsite.shape
    row_base, col_base = bases(rows, cols, gx, gy)
    table = table_lanes(table_ref, table_ref.shape[0])
    row_part = row_envelope(0, rows, row_base, centre_ref[0, 0], extents[0])
    lane = lane_of((rows, LANES))
    for last, out_ref in ((False, west_ref), (True, east_ref)):
        tile = cols // LANES - 1 if last else 0
        envelope = row_part * column_envelope(tile, col_base, centre_ref[0, 1], extents[1])
        values = fields_of((re, im, onsite, down, right), table, (0, rows), tile, envelope)
        packed = jnp.zeros((rows, LANES), jnp.float32)
        for index, value in enumerate(values):
            if last:
                moved = pltpu.roll(value, (LANES - GAP * index) % LANES, 1)
                inside = (lane >= LANES - REACH - GAP * index) & (lane < LANES - GAP * index)
            else:
                moved = pltpu.roll(value, GAP * index, 1)
                inside = (lane >= GAP * index) & (lane < GAP * index + REACH)
            packed = jnp.where(inside, moved, packed)
        out_ref[...] = packed


def halo_columns(from_west, from_east, index):
    lane = lane_of(from_west.shape)
    right = pltpu.roll(from_east, (LANES - GAP * index) % LANES, 1)
    left = pltpu.roll(from_west, GAP * index, 1)
    return jnp.where(lane < REACH, right, jnp.where(lane >= LANES - REACH, left, 0.0))


def rows_kernel(gx, gy, extents, table_ref, centre_ref, re, im, onsite, down, right, from_west, from_east, up_ref, down_out_ref):
    rows, cols = onsite.shape
    row_base, col_base = bases(rows, cols, gx, gy)
    table = table_lanes(table_ref, table_ref.shape[0])
    tiles = cols // LANES
    for first, out_ref in ((0, up_ref), (rows - REACH, down_out_ref)):
        row_part = row_envelope(first, REACH, row_base, centre_ref[0, 0], extents[0])
        for tile in range(tiles + 1):
            if tile == tiles:
                west, east = (r[first : first + REACH, :] for r in (from_west, from_east))
                values = [halo_columns(west, east, index) for index in range(FIELDS)]
            else:
                envelope = row_part * column_envelope(tile, col_base, centre_ref[0, 1], extents[1])
                values = fields_of((re, im, onsite, down, right), table, (first, first + REACH), tile, envelope)
            for index, value in enumerate(values):
                out_ref[index * REACH : (index + 1) * REACH, tile * LANES : (tile + 1) * LANES] = value


def bessel_weights(duration):
    halved = jnp.full((8, LANES), duration * (SPECTRAL * 0.5), jnp.float32)
    square = -(halved * halved)
    weights = []
    power = jnp.ones((8, LANES), jnp.float32)
    for degree in range(TERMS):
        series = jnp.ones((8, LANES), jnp.float32)
        for counter in range(23, 0, -1):
            series = 1.0 + series * (square * (1.0 / (counter * (counter + degree))))
        scale = (1.0 if degree == 0 else 2.0) / math.factorial(degree)
        weights.append(series * power * scale)
        power = power * halved
    return weights


def main_kernel(gx, gy, extents, copies, table_ref, centre_ref, duration_ref, re, im, onsite, down, right,
                from_west, from_east, from_up, from_down, out_re, out_im, sums_ref,
                psi, odd, even, total, coeffs, up_left, weight_ref, norm_ref):
    rows, cols = onsite.shape
    tiles = cols // LANES
    row_base, col_base = bases(rows, cols, gx, gy)
    table = table_lanes(table_ref, table_ref.shape[0])
    own = PAD + TOP
    scales = (1.0, 1.0, 2.0 / SPECTRAL, -2.0 / SPECTRAL, -2.0 / SPECTRAL)
    targets = [psi.at[0], psi.at[1], coeffs.at[0], coeffs.at[1], coeffs.at[2]]

    for degree, weight in enumerate(bessel_weights(duration_ref[0])):
        weight_ref[degree] = weight

    row_part = row_envelope(0, rows, row_base, centre_ref[0, 0], extents[0])
    for tile in range(tiles + 1):
        if tile == tiles:
            values = [halo_columns(from_west[...], from_east[...], index) for index in range(FIELDS)]
        else:
            envelope = row_part * column_envelope(tile, col_base, centre_ref[0, 1], extents[1])
            values = fields_of((re, im, onsite, down, right), table, (0, rows), tile, envelope)
        for value, target, scale in zip(values, targets, scales):
            target[tile, own : own + rows, :] = value if scale == 1.0 else value * scale
        for index, (target, scale) in enumerate(zip(targets, scales)):
            for source, start in ((from_up, own - REACH), (from_down, own + rows)):
                value = source[index * REACH : (index + 1) * REACH, tile * LANES : (tile + 1) * LANES]
                target[tile, start : start + REACH, :] = value if scale == 1.0 else value * scale

    lane = lane_of((8, LANES))
    count = rows // 8
    first_core = TOP // 8
    every = list(range(count + 4))

    def west_of(tile):
        return jnp.where(tile == 0, tiles, tile - 1)

    def east_of(tile):
        return jnp.where(tile == tiles, 0, tile + 1)

    def shift_coeffs(tile, carry):
        other = west_of(tile)
        for block in every:
            at = pl.ds(PAD + 8 * block, 8)
            up_left[0, tile, at, :] = coeffs[1, tile, pl.ds(PAD + 8 * block - 1, 8), :]
            joined = jnp.where(lane == LANES - 1, coeffs[2, other, at, :], coeffs[2, tile, at, :])
            up_left[1, tile, at, :] = pltpu.roll(joined, 1, 1)
        return carry

    lax.fori_loop(0, tiles + 1, shift_coeffs, 0)

    def apply(step, degree, current, previous, target):
        level = step * (TERMS - 1) + degree
        blocks = [b for b in every
                  if 8 * (b + 1) - TOP > level - REACH and 8 * b - TOP < rows + REACH - level]
        wanted = [b for b in every
                  if 8 * (b + 1) - TOP > -(REACH - TERMS + 1) and 8 * b - TOP < rows + REACH - TERMS + 1]
        core = list(range(first_core, first_core + count))
        last_step = step == STEPS - 1

        def body(tile, carry):
            before, norm, norm_zero = carry
            west, east = west_of(tile), east_of(tile)
            squares = None
            zero_squares = None
            for block in blocks:
                at = pl.ds(PAD + 8 * block, 8)
                pot, hop_d, hop_r = (coeffs[k, tile, at, :] for k in range(3))
                hop_u, hop_l = (up_left[k, tile, at, :] for k in range(2))
                found = []
                for part in range(2):
                    centre = current[part, tile, at, :]
                    below = current[part, tile, pl.ds(PAD + 8 * block + 1, 8), :]
                    above = current[part, tile, pl.ds(PAD + 8 * block - 1, 8), :]
                    left = pltpu.roll(jnp.where(lane == LANES - 1, current[part, west, at, :], centre), 1, 1)
                    right_ = pltpu.roll(jnp.where(lane == 0, current[part, east, at, :], centre), LANES - 1, 1)
                    applied = (pot * centre + hop_d * below) + (hop_u * above + hop_r * right_) + hop_l * left
                    if degree == 1:
                        following = 0.5 * applied
                    else:
                        following = applied - previous[part, tile, at, :]
                    target[part, tile, at, :] = following
                    found.append(following)
                keep = core if last_step else wanted
                if block in keep:
                    quarter = degree % 4
                    first, second = (found[0], found[1]) if quarter % 2 == 0 else (found[1], found[0])
                    weight = weight_ref[degree]
                    adds = (first * weight, second * weight)
                    signs = {0: (1, 1), 1: (1, -1), 2: (-1, -1), 3: (-1, 1)}[quarter]
                    for part in range(2):
                        if degree == 1:
                            base = current[part, tile, at, :] * weight_ref[0]
                        elif last_step:
                            base = even_total[part, tile, pl.ds(PAD + 8 * block, 8), :]
                        else:
                            base = total[part, tile, at, :]
                        value = base + adds[part] if signs[part] > 0 else base - adds[part]
                        if last_step:
                            even_total[part, tile, at, :] = value
                        else:
                            total[part, tile, at, :] = value
                if block in core:
                    for part in range(2):
                        square = found[part] * found[part]
                        squares = square if squares is None else squares + square
                        if degree == 1:
                            start = current[part, tile, at, :]
                            start = start * start
                            zero_squares = start if zero_squares is None else zero_squares + start
            norm = norm + jnp.where(tile < tiles, squares, 0.0)
            if degree == 1:
                norm_zero = norm_zero + jnp.where(tile < tiles, zero_squares, 0.0)
            return before, norm, norm_zero

        zero = jnp.zeros((8, LANES), jnp.float32)
        _, norm, norm_zero = lax.fori_loop(0, tiles + 1, body, (0, zero, zero))
        norm_ref[step * TERMS + degree] = norm
        if degree == 1:
            norm_ref[step * TERMS] = norm_zero

    even_total = psi
    for step in range(STEPS):
        start = psi if step == 0 else total
        sequence = [start, odd, even]
        apply(step, 1, start, None, odd)
        apply(step, 2, odd, start, even)
        for degree in range(3, TERMS):
            if degree % 2:
                apply(step, degree, even, odd, odd)
            else:
                apply(step, degree, odd, even, even)
        source = total if step < STEPS - 1 else even_total
        square = jnp.zeros((8, LANES), jnp.float32)
        for tile in range(tiles):
            for block in range(first_core, first_core + count):
                for part in range(2):
                    value = source[part, tile, pl.ds(PAD + 8 * block, 8), :]
                    square = square + value * value
                    if step == STEPS - 1:
                        out_ref = (out_re, out_im)[part]
                        out_ref[8 * (block - first_core) : 8 * (block - first_core) + 8, tile * LANES : (tile + 1) * LANES] = value
        norm_ref[STEPS * TERMS + step] = square

    lane_row = lane_of((1, LANES))
    packed = jnp.zeros((1, LANES), jnp.float32)
    for index in range(STEPS * TERMS + STEPS):
        found = jnp.sum(jnp.sum(norm_ref[index], axis=0, keepdims=True), axis=1, keepdims=True)
        packed = jnp.where(lane_row == index, found, packed)
    sums_ref[...] = jnp.broadcast_to(packed, (copies, LANES))


def scale_kernel(cell_count, totals_ref, re_ref, im_ref, out_re, out_im, norms_ref):
    totals = jnp.sum(totals_ref[...], axis=0, keepdims=True) * (1.0 / cell_count)
    lane = lane_of(totals.shape)
    factor = jnp.ones((1, 1), jnp.float32)
    for step in range(STEPS):
        squared = factor * factor
        moved = totals if step == 0 else pltpu.roll(totals, LANES - step * TERMS, 1)
        norms_ref[step] = (moved * squared)[:, :TERMS]
        mean = jnp.sum(jnp.where(lane == STEPS * TERMS + step, totals, 0.0), axis=1, keepdims=True) * squared
        factor = factor * lax.rsqrt(mean + EPSILON)
    out_re[0] = re_ref[...] * factor
    out_im[0] = im_ref[...] * factor


def neighbours(block_low, block_high, axis, count):
    forward = [(i, (i + 1) % count) for i in range(count)]
    backward = [(target, source) for source, target in forward]
    from_previous = lax.ppermute(block_high, axis, forward)
    from_next = lax.ppermute(block_low, axis, backward)
    return from_previous, from_next


def grant(mebibytes):
    return pltpu.CompilerParams(vmem_limit_bytes=mebibytes * 2**20)


def vmem_specs(count):
    return [pl.BlockSpec(memory_space=VMEM)] * count


def per_device(gx, gy, counts, interpret, init_re, init_im, onsite, bond_x, bond_y, hop_table, centre, duration):
    rows, cols = onsite.shape
    extents = (rows * counts[0], cols * counts[1])
    tiles = cols // LANES
    both = gx + gy
    everyone = counts[0] * counts[1]
    smem = [pl.BlockSpec(memory_space=SMEM)]
    local = (init_re, init_im, onsite, bond_x, bond_y)
    shape = lambda *s: jax.ShapeDtypeStruct(s, jnp.float32)
    height = rows + 2 * TOP + 2 * PAD

    west, east = pl.pallas_call(
        functools.partial(strip_kernel, gx, gy, extents),
        out_shape=[shape(rows, LANES)] * 2,
        in_specs=smem * 2 + vmem_specs(5), out_specs=vmem_specs(2), interpret=interpret, name="strips", compiler_params=grant(4),
    )(hop_table, centre, *local)
    from_west, from_east = neighbours(west, east, gy, counts[1])
    packed_rows = -(-FIELDS * REACH // 8) * 8
    up, down = pl.pallas_call(
        functools.partial(rows_kernel, gx, gy, extents),
        out_shape=[shape(packed_rows, cols + LANES)] * 2,
        in_specs=smem * 2 + vmem_specs(7), out_specs=vmem_specs(2), interpret=interpret, name="rows", compiler_params=grant(8),
    )(hop_table, centre, *local, from_west, from_east)
    from_up, from_down = neighbours(up, down, gx, counts[0])
    panel = lambda n: pltpu.VMEM((n, tiles + 1, height, LANES), jnp.float32)
    acc_re, acc_im, sums = pl.pallas_call(
        functools.partial(main_kernel, gx, gy, extents, everyone),
        out_shape=[shape(rows, cols), shape(rows, cols), shape(everyone, LANES)],
        in_specs=smem * 3 + vmem_specs(9), out_specs=vmem_specs(3),
        scratch_shapes=[panel(2), panel(2), panel(2), panel(2), panel(3), panel(2),
                        pltpu.VMEM((TERMS, 8, LANES), jnp.float32),
                        pltpu.VMEM((STEPS * TERMS + STEPS, 8, LANES), jnp.float32)],
        interpret=interpret, name="chebyshev", compiler_params=grant(20),
    )(hop_table, centre, duration, *local, from_west, from_east, from_up, from_down)
    totals = lax.all_to_all(sums, both, 0, 0, tiled=True)
    out_re, out_im, norms = pl.pallas_call(
        functools.partial(scale_kernel, extents[0] * extents[1]),
        out_shape=[shape(1, rows, cols), shape(1, rows, cols), shape(STEPS, 1, TERMS)],
        in_specs=vmem_specs(3), out_specs=vmem_specs(3), interpret=interpret, name="scale", compiler_params=grant(4),
    )(totals, acc_re, acc_im)
    return out_re, out_im, jnp.swapaxes(norms, 1, 2)


def solution(mesh, interpret=False):
    gx, gy = ("gx",), ("gy",)
    counts = (mesh.shape["gx"], mesh.shape["gy"])
    whole, plane = P(None, "gx", "gy"), P("gx", "gy")
    return jax.shard_map(
        functools.partial(per_device, gx, gy, counts, interpret),
        mesh=mesh,
        in_specs=(whole, whole, plane, plane, plane, P(), P(), P()),
        out_specs=(whole, whole, P()),
        check_vma=False,
    )
```

time: 155 us -> 88.7 us (0.57)
  the two profiles are of different devices: /device:TPU:2 before, /device:TPU:1 now
where the time goes in v1:
time: 88.7 us; the launch traced here: 88.4 us
  blocking collectives  35.1 us (40%)
  starting transfers between devices  19.2 us (22%)
  Pallas kernels  17.8 us (20%)
  waiting for transfers between devices  9.04 us (10%)
  local copies, waits for them, and re-layouts  5.85 us (7%)
  between operations  1.42 us (2%)
    all_to_all x1, blocking collectives, per_device(): totals = lax.all_to_all(sums, both, 0, 0, tiled=True)  35.1 us
    pallas_call x1, Pallas kernels, per_device(): pl.pallas_call(functools.partial(main_kernel, gx, gy, extents, everyone),...  15.4 us
    ppermute x2, starting transfers between devices, neighbours(): from_previous = lax.ppermute(block_high, axis, forward)  9.73 us
    ppermute x2, starting transfers between devices, neighbours(): from_next = lax.ppermute(block_low, axis, backward)  9.46 us
    ppermute x2, waiting for transfers between devices, neighbours(): from_next = lax.ppermute(block_low, axis, backward)  9.03 us
    unnamed x28, local copies, waits for them, and re-layouts  5.85 us
  transfers between devices with their start and end apart: 4, of which 2 were waited for; matrix products, arithmetic and copies ran while one was open for 0% of the time, Pallas kernels for 0%

profile of v1, /device:TPU:1, one launch (start us, length us, event | category | flops | bytes accessed | tf_op | source)
XLA Modules:
  0.0 88.4 jit_solution(738474633033222868)
XLA Ops:
  0.6 0.0 copy-start
  0.6 0.9 %copy-done = f32[1,32,1024]{2,1,0:T(8,128)S(1)} copy-done((f32[1,32,1024]{2,1,0:T(8,128)S(1)}, f32[1,32,1024]{2,1,0:T(8,128)}, u32[]{:S(2)}) %copy-start) | copy-done | bytes 131096
  1.5 0.0 copy-start.2
  1.5 0.9 %copy-done.2 = f32[1,32,1024]{2,1,0:T(8,128)S(1)} copy-done((f32[1,32,1024]{2,1,0:T(8,128)S(1)}, f32[1,32,1024]{2,1,0:T(8,128)}, u32[]{:S(2)}) %copy-start.2) | copy-done | bytes 131096
  2.4 0.0 copy-start.4
  2.4 0.9 %copy-done.4 = f32[32,1024]{1,0:T(8,128)S(1)} copy-done((f32[32,1024]{1,0:T(8,128)S(1)}, f32[32,1024]{1,0:T(8,128)}, u32[]{:S(2)}) %copy-start.4) | copy-done | bytes 131096
  3.3 0.0 copy-start.6
  3.3 0.9 %copy-done.6 = s32[32,1024]{1,0:T(8,128)S(1)} copy-done((s32[32,1024]{1,0:T(8,128)S(1)}, s32[32,1024]{1,0:T(8,128)}, u32[]{:S(2)}) %copy-start.6) | copy-done | bytes 131096
  4.3 0.0 copy-start.8
  4.3 0.9 %copy-done.8 = s32[32,1024]{1,0:T(8,128)S(1)} copy-done((s32[32,1024]{1,0:T(8,128)S(1)}, s32[32,1024]{1,0:T(8,128)}, u32[]{:S(2)}) %copy-start.8) | copy-done | bytes 131096
  5.2 0.0 copy-start.10
  5.2 0.7 copy-done.10
  5.8 0.0 copy-start.12
  5.8 0.7 copy-done.12
  6.5 0.0 copy-start.1
  6.5 0.0 copy-start.3
  6.5 0.0 copy-start.5
  6.5 0.0 copy-start.7
  6.5 0.0 copy-start.9
  6.5 0.7 strips.1
  7.2 0.0 copy-start.11
  7.2 0.0 copy-start.13
  7.2 3.9 %collective-permute-start = (f32[32,128]{1,0:T(8,128)S(1)}, f32[32,128]{1,0:T(8,128)S(1)}, u32[]{:S(2)}, u32[]{:S(2)}) collective-permute-start(f32[32,128]{1,0:T(8,128)S(1)} %get-tuple-element.13), channel_id=1, source_target_pairs={{0,1},{1,2},{2,3},{3,4},{4,5},{5,6},{6,7},{7,8},{8,9},{9,10},{10,1... | collective-permute-start | bytes 49160 | tf_op jit(solution)/shard_map/ppermute | solution.py:306
  11.2 4.8 %collective-permute-start.1 = (f32[32,128]{1,0:T(8,128)S(1)}, f32[32,128]{1,0:T(8,128)S(1)}, u32[]{:S(2)}, u32[]{:S(2)}) collective-permute-start(f32[32,128]{1,0:T(8,128)S(1)} %get-tuple-element.14), channel_id=1, source_target_pairs={{1,0},{2,1},{3,2},{4,3},{5,4},{6,5},{7,6},{8,7},{9,8},{10,9},{11,1... | collective-permute-start | bytes 49160 | tf_op jit(solution)/shard_map/ppermute | solution.py:307
  16.0 0.0 collective-permute-done.from_west
  16.0 0.8 collective-permute-done.1.from_east
  16.9 0.0 copy-done.1
  16.9 0.0 copy-done.3
  16.9 0.0 copy-done.5
  16.9 0.0 copy-done.7
  16.9 0.0 copy-done.9
  16.9 0.0 copy-done.11
  16.9 0.0 copy-done.13
  16.9 0.8 rows.1
  17.7 5.8 %collective-permute-start.2 = (f32[72,1152]{1,0:T(8,128)S(1)}, f32[72,1152]{1,0:T(8,128)S(1)}, u32[]{:S(2)}, u32[]{:S(2)}) collective-permute-start(f32[72,1152]{1,0:T(8,128)S(1)} %get-tuple-element.15), channel_id=1, source_target_pairs={{0,16},{16,32},{32,48},{48,64},{64,80},{80,96},{96,112},{112,128},... | collective-permute-start | bytes 995336 | tf_op jit(solution)/shard_map/ppermute | solution.py:306
  23.5 4.6 %collective-permute-start.3 = (f32[72,1152]{1,0:T(8,128)S(1)}, f32[72,1152]{1,0:T(8,128)S(1)}, u32[]{:S(2)}, u32[]{:S(2)}) collective-permute-start(f32[72,1152]{1,0:T(8,128)S(1)} %get-tuple-element.16), channel_id=1, source_target_pairs={{16,0},{32,16},{48,32},{64,48},{80,64},{96,80},{112,96},{128,112},... | collective-permute-start | bytes 995336 | tf_op jit(solution)/shard_map/ppermute | solution.py:307
  28.8 0.0 collective-permute-done.2.from_up
  28.8 8.2 %collective-permute-done.3.from_down = f32[72,1152]{1,0:T(8,128)S(1)} collective-permute-done((f32[72,1152]{1,0:T(8,128)S(1)}, f32[72,1152]{1,0:T(8,128)S(1)}, u32[]{:S(2)}, u32[]{:S(2)}) %collective-permute-start.3) | collective-permute-done | bytes 331808 | tf_op jit(solution)/shard_map/ppermute | solution.py:307
  37.0 15.4 %chebyshev.1 = (f32[32,1024]{1,0:T(8,128)S(1)}, f32[32,1024]{1,0:T(8,128)S(1)}, f32[512,128]{1,0:T(8,128)S(1)}) custom-call(f32[16]{0:T(128)S(1)} %copy-done.11, s32[1,2]{1,0:T(1,128)S(1)} %copy-done.13, f32[1]{0:T(128)S(6)} %copy.14.duration_ref, f32[1,32,1024]{2,1,0:T(8,128)S(1)} %copy-done.1, f32[1,32,1024]{2,1,0:T(8,128)S(1)} %copy-done.3, ...), custom_call_target="tpu_custom_call" | custom-call | tf_op jit(solution)/shard_map/chebyshev/pallas_call | solution.py:344
  52.4 35.1 %all_to_all.11 = f32[512,1,128]{2,1,0:T(1,128)S(1)} all-to-all(f32[512,1,128]{2,1,0:T(1,128)S(1)} %bitcast.8), channel_id=1, replica_groups=mesh['gx'=32,'gy'=16] {'gx','gy'}, dimensions={0} | all-to-all | bytes 524288 | tf_op jit(solution)/shard_map/all_to_all | solution.py:353
  87.5 0.9 scale.1
Async XLA Ops:
  0.6 0.9 %copy-start = (f32[1,32,1024]{2,1,0:T(8,128)S(1)}, f32[1,32,1024]{2,1,0:T(8,128)}, u32[]{:S(2)}) copy-start(f32[1,32,1024]{2,1,0:T(8,128)} %re.5) | copy-start | bytes 393220
  1.5 0.9 %copy-start.2 = (f32[1,32,1024]{2,1,0:T(8,128)S(1)}, f32[1,32,1024]{2,1,0:T(8,128)}, u32[]{:S(2)}) copy-start(f32[1,32,1024]{2,1,0:T(8,128)} %im.5) | copy-start | bytes 393220
  2.4 0.9 %copy-start.4 = (f32[32,1024]{1,0:T(8,128)S(1)}, f32[32,1024]{1,0:T(8,128)}, u32[]{:S(2)}) copy-start(f32[32,1024]{1,0:T(8,128)} %onsite.5) | copy-start | bytes 393220
  3.3 0.9 %copy-start.6 = (s32[32,1024]{1,0:T(8,128)S(1)}, s32[32,1024]{1,0:T(8,128)}, u32[]{:S(2)}) copy-start(s32[32,1024]{1,0:T(8,128)} %down.5) | copy-start | bytes 393220
  4.3 0.9 %copy-start.8 = (s32[32,1024]{1,0:T(8,128)S(1)}, s32[32,1024]{1,0:T(8,128)}, u32[]{:S(2)}) copy-start(s32[32,1024]{1,0:T(8,128)} %right.5) | copy-start | bytes 393220
  5.2 0.7 copy-start.10
  5.8 0.7 copy-start.12
  6.5 10.4 %copy-start.1 = (f32[1,32,1024]{2,1,0:T(8,128)S(1)}, f32[1,32,1024]{2,1,0:T(8,128)}, u32[]{:S(2)}) copy-start(f32[1,32,1024]{2,1,0:T(8,128)} %re.5) | copy-start | bytes 393220
  6.5 10.4 %copy-start.3 = (f32[1,32,1024]{2,1,0:T(8,128)S(1)}, f32[1,32,1024]{2,1,0:T(8,128)}, u32[]{:S(2)}) copy-start(f32[1,32,1024]{2,1,0:T(8,128)} %im.5) | copy-start | bytes 393220
  6.5 10.4 %copy-start.5 = (f32[32,1024]{1,0:T(8,128)S(1)}, f32[32,1024]{1,0:T(8,128)}, u32[]{:S(2)}) copy-start(f32[32,1024]{1,0:T(8,128)} %onsite.5) | copy-start | bytes 393220
  6.5 10.4 %copy-start.7 = (s32[32,1024]{1,0:T(8,128)S(1)}, s32[32,1024]{1,0:T(8,128)}, u32[]{:S(2)}) copy-start(s32[32,1024]{1,0:T(8,128)} %down.5) | copy-start | bytes 393220
  6.5 10.4 %copy-start.9 = (s32[32,1024]{1,0:T(8,128)S(1)}, s32[32,1024]{1,0:T(8,128)}, u32[]{:S(2)}) copy-start(s32[32,1024]{1,0:T(8,128)} %right.5) | copy-start | bytes 393220
  7.2 9.7 %copy-start.11 = (f32[16]{0:T(128)S(1)}, f32[16]{0:T(128)}, u32[]{:S(2)}) copy-start(f32[16]{0:T(128)} %table_ref.5) | copy-start | bytes 196
  7.2 9.7 %copy-start.13 = (s32[1,2]{1,0:T(1,128)S(1)}, s32[1,2]{1,0:T(1,128)}, u32[]{:S(2)}) copy-start(s32[1,2]{1,0:T(1,128)} %centre_ref.5) | copy-start | bytes 28
  7.2 8.8 %collective-permute-start = (f32[32,128]{1,0:T(8,128)S(1)}, f32[32,128]{1,0:T(8,128)S(1)}, u32[]{:S(2)}, u32[]{:S(2)}) collective-permute-start(f32[32,128]{1,0:T(8,128)S(1)} %get-tuple-element.13), channel_id=1, source_target_pairs={{0,1},{1,2},{2,3},{3,4},{4,5},{5,6},{6,7},{7,8},{8,9},{9,10},{10,1... | collective-permute-start | bytes 49160 | tf_op jit(solution)/shard_map/ppermute | solution.py:306
  11.2 5.7 %collective-permute-start.1 = (f32[32,128]{1,0:T(8,128)S(1)}, f32[32,128]{1,0:T(8,128)S(1)}, u32[]{:S(2)}, u32[]{:S(2)}) collective-permute-start(f32[32,128]{1,0:T(8,128)S(1)} %get-tuple-element.14), channel_id=1, source_target_pairs={{1,0},{2,1},{3,2},{4,3},{5,4},{6,5},{7,6},{8,7},{9,8},{10,9},{11,1... | collective-permute-start | bytes 49160 | tf_op jit(solution)/shard_map/ppermute | solution.py:307
  17.7 11.1 %collective-permute-start.2 = (f32[72,1152]{1,0:T(8,128)S(1)}, f32[72,1152]{1,0:T(8,128)S(1)}, u32[]{:S(2)}, u32[]{:S(2)}) collective-permute-start(f32[72,1152]{1,0:T(8,128)S(1)} %get-tuple-element.15), channel_id=1, source_target_pairs={{0,16},{16,32},{32,48},{48,64},{64,80},{80,96},{96,112},{112,128},... | collective-permute-start | bytes 995336 | tf_op jit(solution)/shard_map/ppermute | solution.py:306
  23.5 13.5 %collective-permute-start.3 = (f32[72,1152]{1,0:T(8,128)S(1)}, f32[72,1152]{1,0:T(8,128)S(1)}, u32[]{:S(2)}, u32[]{:S(2)}) collective-permute-start(f32[72,1152]{1,0:T(8,128)S(1)} %get-tuple-element.16), channel_id=1, source_target_pairs={{16,0},{32,16},{48,32},{64,48},{80,64},{96,80},{112,96},{128,112},... | collective-permute-start | bytes 995336 | tf_op jit(solution)/shard_map/ppermute | solution.py:307

commit v2 on v1

--- a/solution.py
+++ b/solution.py
@@ -18,6 +18,7 @@
 PAD = 8
 TOP = 16
 FIELDS = 5
+UNROLL = 9
 VMEM = pltpu.VMEM
 SMEM = pltpu.SMEM
 
@@ -61,38 +62,66 @@
     return lax.axis_index(gx) * rows, lax.axis_index(gy) * cols
 
 
-def fields_of(refs, table, rows, tile, envelope):
-    re_ref, im_ref, onsite_ref, down_ref, right_ref = refs
-    cut = (slice(*rows), pl.ds(tile * LANES, LANES))
-    return [
-        re_ref[0, cut[0], cut[1]] * envelope,
-        im_ref[0, cut[0], cut[1]] * envelope,
-        onsite_ref[cut],
-        looked_up(table, down_ref[cut]),
-        looked_up(table, right_ref[cut]),
+def fields_kernel(gx, gy, extents, table_hbm, centre_hbm, re, im, onsite, down, right, fields_ref, near_ref, far_ref,
+                  table_ref, centre_ref, fine, codes, sems):
+    rows, cols = onsite.shape
+    copies = [
+        (table_hbm, table_ref),
+        (centre_hbm, centre_ref),
+        (re.at[0], fine.at[0]),
+        (im.at[0], fine.at[1]),
+        (down, codes.at[0]),
+        (right, codes.at[1]),
+        (onsite, fields_ref.at[2]),
     ]
-
-
-def strip_kernel(gx, gy, extents, table_ref, centre_ref, re, im, onsite, down, right, west_ref, east_ref):
-    rows, cols = onsite.shape
+    started = [pltpu.make_async_copy(source, target, sems.at[i]) for i, (source, target) in enumerate(copies)]
+    for copy in started:
+        copy.start()
+    for copy in started:
+        copy.wait()
     row_base, col_base = bases(rows, cols, gx, gy)
     table = table_lanes(table_ref, table_ref.shape[0])
     row_part = row_envelope(0, rows, row_base, centre_ref[0, 0], extents[0])
     lane = lane_of((rows, LANES))
-    for last, out_ref in ((False, west_ref), (True, east_ref)):
-        tile = cols // LANES - 1 if last else 0
+    tiles = cols // LANES
+    packs = []
+    for tile in (0, tiles - 1, *range(1, tiles - 1)):
+        cut = slice(tile * LANES, (tile + 1) * LANES)
         envelope = row_part * column_envelope(tile, col_base, centre_ref[0, 1], extents[1])
-        values = fields_of((re, im, onsite, down, right), table, (0, rows), tile, envelope)
+        values = [
+            fine[0, :, cut] * envelope,
+            fine[1, :, cut] * envelope,
+            fields_ref[2, :, cut],
+            looked_up(table, codes[0, :, cut]),
+            looked_up(table, codes[1, :, cut]),
+        ]
+        for index in (0, 1, 3, 4):
+            fields_ref[index, :, cut] = values[index]
+        if 0 < tile < tiles - 1:
+            continue
         packed = jnp.zeros((rows, LANES), jnp.float32)
         for index, value in enumerate(values):
-            if last:
+            if tile:
                 moved = pltpu.roll(value, (LANES - GAP * index) % LANES, 1)
                 inside = (lane >= LANES - REACH - GAP * index) & (lane < LANES - GAP * index)
             else:
                 moved = pltpu.roll(value, GAP * index, 1)
                 inside = (lane >= GAP * index) & (lane < GAP * index + REACH)
             packed = jnp.where(inside, moved, packed)
-        out_ref[...] = packed
+        packs.append(packed)
+    west, east = packs
+    odd = lax.rem(lax.axis_index(gy), 2) == 1
+    near_ref[...] = jnp.where(odd, west, east)
+    far_ref[...] = jnp.where(odd, east, west)
+
+
+def strips_from(gy, near_ref, far_ref):
+    rows = far_ref.shape[0]
+    parity = lax.rem(lax.axis_index(gy), 2)
+    near = near_ref[pl.ds(pl.multiple_of((1 - parity) * rows, 8), rows), :]
+    far = far_ref[...]
+    odd = parity == 1
+    return jnp.where(odd, near, far), jnp.where(odd, far, near)
 
 
 def halo_columns(from_west, from_east, index):
@@ -102,22 +131,27 @@
     return jnp.where(lane < REACH, right, jnp.where(lane >= LANES - REACH, left, 0.0))
 
 
-def rows_kernel(gx, gy, extents, table_ref, centre_ref, re, im, onsite, down, right, from_west, from_east, up_ref, down_out_ref):
-    rows, cols = onsite.shape
-    row_base, col_base = bases(rows, cols, gx, gy)
-    table = table_lanes(table_ref, table_ref.shape[0])
-    tiles = cols // LANES
-    for first, out_ref in ((0, up_ref), (rows - REACH, down_out_ref)):
-        row_part = row_envelope(first, REACH, row_base, centre_ref[0, 0], extents[0])
-        for tile in range(tiles + 1):
-            if tile == tiles:
-                west, east = (r[first : first + REACH, :] for r in (from_west, from_east))
-                values = [halo_columns(west, east, index) for index in range(FIELDS)]
-            else:
-                envelope = row_part * column_envelope(tile, col_base, centre_ref[0, 1], extents[1])
-                values = fields_of((re, im, onsite, down, right), table, (first, first + REACH), tile, envelope)
-            for index, value in enumerate(values):
-                out_ref[index * REACH : (index + 1) * REACH, tile * LANES : (tile + 1) * LANES] = value
+def rows_kernel(gx, gy, fields_ref, near_strip, far_strip, near_ref, far_ref):
+    _, rows, cols = fields_ref.shape
+    from_west, from_east = strips_from(gy, near_strip, far_strip)
+    parity = lax.rem(lax.axis_index(gx), 2)
+
+    def fill(first, out_ref):
+        west, east = (r[first : first + REACH, :] for r in (from_west, from_east))
+        for index in range(FIELDS):
+            at = slice(index * REACH, (index + 1) * REACH)
+            out_ref[at, cols : cols + LANES] = halo_columns(west, east, index)
+            out_ref[at, :cols] = fields_ref[index, first : first + REACH, :]
+
+    @pl.when(parity == 0)
+    def _():
+        fill(0, far_ref)
+        fill(rows - REACH, near_ref)
+
+    @pl.when(parity == 1)
+    def _():
+        fill(0, near_ref)
+        fill(rows - REACH, far_ref)
 
 
 def bessel_weights(duration):
@@ -135,13 +169,11 @@
     return weights
 
 
-def main_kernel(gx, gy, extents, copies, table_ref, centre_ref, duration_ref, re, im, onsite, down, right,
-                from_west, from_east, from_up, from_down, out_re, out_im, sums_ref,
+def main_kernel(gx, gy, copies, duration_ref, fields_ref,
+                near_strip, far_strip, near_rows, far_rows, out_re, out_im, sums_ref,
                 psi, odd, even, total, coeffs, up_left, weight_ref, norm_ref):
-    rows, cols = onsite.shape
+    _, rows, cols = fields_ref.shape
     tiles = cols // LANES
-    row_base, col_base = bases(rows, cols, gx, gy)
-    table = table_lanes(table_ref, table_ref.shape[0])
     own = PAD + TOP
     scales = (1.0, 1.0, 2.0 / SPECTRAL, -2.0 / SPECTRAL, -2.0 / SPECTRAL)
     targets = [psi.at[0], psi.at[1], coeffs.at[0], coeffs.at[1], coeffs.at[2]]
@@ -149,19 +181,34 @@
     for degree, weight in enumerate(bessel_weights(duration_ref[0])):
         weight_ref[degree] = weight
 
-    row_part = row_envelope(0, rows, row_base, centre_ref[0, 0], extents[0])
-    for tile in range(tiles + 1):
-        if tile == tiles:
-            values = [halo_columns(from_west[...], from_east[...], index) for index in range(FIELDS)]
-        else:
-            envelope = row_part * column_envelope(tile, col_base, centre_ref[0, 1], extents[1])
-            values = fields_of((re, im, onsite, down, right), table, (0, rows), tile, envelope)
-        for value, target, scale in zip(values, targets, scales):
+    from_west, from_east = strips_from(gy, near_strip, far_strip)
+    for index, (target, scale) in enumerate(zip(targets, scales)):
+        for tile in range(tiles + 1):
+            if tile == tiles:
+                value = halo_columns(from_west, from_east, index)
+            else:
+                value = fields_ref[index, :, tile * LANES : (tile + 1) * LANES]
             target[tile, own : own + rows, :] = value if scale == 1.0 else value * scale
-        for index, (target, scale) in enumerate(zip(targets, scales)):
-            for source, start in ((from_up, own - REACH), (from_down, own + rows)):
-                value = source[index * REACH : (index + 1) * REACH, tile * LANES : (tile + 1) * LANES]
-                target[tile, start : start + REACH, :] = value if scale == 1.0 else value * scale
+
+    packed_rows = far_rows.shape[0]
+
+    def place(from_up, from_down):
+        for source, base, start in ((*from_up, own - REACH), (*from_down, own + rows)):
+            for index, (target, scale) in enumerate(zip(targets, scales)):
+                first = base + index * REACH
+                for tile in range(tiles + 1):
+                    value = source[first : first + REACH, tile * LANES : (tile + 1) * LANES]
+                    target[tile, start : start + REACH, :] = value if scale == 1.0 else value * scale
+
+    row_parity = lax.rem(lax.axis_index(gx), 2)
+
+    @pl.when(row_parity == 0)
+    def _():
+        place((far_rows, 0), (near_rows, packed_rows))
+
+    @pl.when(row_parity == 1)
+    def _():
+        place((near_rows, 0), (far_rows, 0))
 
     lane = lane_of((8, LANES))
     count = rows // 8
@@ -169,9 +216,13 @@
     every = list(range(count + 4))
 
     def west_of(tile):
+        if isinstance(tile, int):
+            return (tile - 1) % (tiles + 1)
         return jnp.where(tile == 0, tiles, tile - 1)
 
     def east_of(tile):
+        if isinstance(tile, int):
+            return (tile + 1) % (tiles + 1)
         return jnp.where(tile == tiles, 0, tile + 1)
 
     def shift_coeffs(tile, carry):
@@ -244,13 +295,29 @@
                             start = current[part, tile, at, :]
                             start = start * start
                             zero_squares = start if zero_squares is None else zero_squares + start
-            norm = norm + jnp.where(tile < tiles, squares, 0.0)
-            if degree == 1:
-                norm_zero = norm_zero + jnp.where(tile < tiles, zero_squares, 0.0)
+            if not isinstance(tile, int):
+                squares = jnp.where(tile < tiles, squares, 0.0)
+                if degree == 1:
+                    zero_squares = jnp.where(tile < tiles, zero_squares, 0.0)
+            if not isinstance(tile, int) or tile < tiles:
+                norm = norm + squares
+                if degree == 1:
+                    norm_zero = norm_zero + zero_squares
             return before, norm, norm_zero
 
         zero = jnp.zeros((8, LANES), jnp.float32)
-        _, norm, norm_zero = lax.fori_loop(0, tiles + 1, body, (0, zero, zero))
+        carry = (0, zero, zero)
+        if UNROLL > tiles:
+            for tile in range(tiles + 1):
+                carry = body(tile, carry)
+        else:
+            def group(index, carry):
+                for offset in range(UNROLL):
+                    carry = body(index * UNROLL + offset, carry)
+                return carry
+
+            carry = lax.fori_loop(0, (tiles + 1) // UNROLL, group, carry)
+        _, norm, norm_zero = carry
         norm_ref[step * TERMS + degree] = norm
         if degree == 1:
             norm_ref[step * TERMS] = norm_zero
@@ -300,12 +367,22 @@
     out_im[0] = im_ref[...] * factor
 
 
-def neighbours(block_low, block_high, axis, count):
-    forward = [(i, (i + 1) % count) for i in range(count)]
-    backward = [(target, source) for source, target in forward]
-    from_previous = lax.ppermute(block_high, axis, forward)
-    from_next = lax.ppermute(block_low, axis, backward)
-    return from_previous, from_next
+def far_pairs(count):
+    pairs = [(i, (i + 1) % count) for i in range(1, count, 2)]
+    return pairs + [(target, source) for source, target in pairs]
+
+
+def near_pairs(count):
+    return [[i, i + 1] for i in range(0, count, 2)]
+
+
+def swapped(near, far, axis, count):
+    from_far = lax.ppermute(far, axis, far_pairs(count))
+    from_near = lax.all_gather(near, axis, axis=0, tiled=True, axis_index_groups=near_pairs(count))
+    return from_near, from_far
+
+
+FIELDS_PARAMS = pltpu.CompilerParams(vmem_limit_bytes=20 * 2**20)
 
 
 def grant(mebibytes):
@@ -316,7 +393,7 @@
     return [pl.BlockSpec(memory_space=VMEM)] * count
 
 
-def per_device(gx, gy, counts, interpret, init_re, init_im, onsite, bond_x, bond_y, hop_table, centre, duration):
+def per_device(gx, gy, counts, init_re, init_im, onsite, bond_x, bond_y, hop_table, centre, duration):
     rows, cols = onsite.shape
     extents = (rows * counts[0], cols * counts[1])
     tiles = cols // LANES
@@ -327,44 +404,48 @@
     shape = lambda *s: jax.ShapeDtypeStruct(s, jnp.float32)
     height = rows + 2 * TOP + 2 * PAD
 
-    west, east = pl.pallas_call(
-        functools.partial(strip_kernel, gx, gy, extents),
-        out_shape=[shape(rows, LANES)] * 2,
-        in_specs=smem * 2 + vmem_specs(5), out_specs=vmem_specs(2), interpret=interpret, name="strips", compiler_params=grant(4),
-    )(hop_table, centre, *local)
-    from_west, from_east = neighbours(west, east, gy, counts[1])
+    hbm = [pl.BlockSpec(memory_space=pltpu.HBM)]
+    fields, near, far = pl.pallas_call(
+        functools.partial(fields_kernel, gx, gy, extents),
+        out_shape=[shape(FIELDS, rows, cols), shape(rows, LANES), shape(rows, LANES)],
+        in_specs=hbm * 7, out_specs=vmem_specs(3),
+        scratch_shapes=[SMEM(hop_table.shape, jnp.float32), SMEM(centre.shape, jnp.int32), VMEM((2, rows, cols), jnp.float32),
+                        VMEM((2, rows, cols), jnp.int32), pltpu.SemaphoreType.DMA((7,))],
+        name="fields", compiler_params=FIELDS_PARAMS,
+    )(*(pltpu.with_memory_space_constraint(x, pltpu.HBM) for x in (hop_table, centre, *local)))
+    near_strip, far_strip = swapped(near, far, gy[0], counts[1])
     packed_rows = -(-FIELDS * REACH // 8) * 8
-    up, down = pl.pallas_call(
-        functools.partial(rows_kernel, gx, gy, extents),
+    near, far = pl.pallas_call(
+        functools.partial(rows_kernel, gx, gy),
         out_shape=[shape(packed_rows, cols + LANES)] * 2,
-        in_specs=smem * 2 + vmem_specs(7), out_specs=vmem_specs(2), interpret=interpret, name="rows", compiler_params=grant(8),
-    )(hop_table, centre, *local, from_west, from_east)
-    from_up, from_down = neighbours(up, down, gx, counts[0])
+        in_specs=vmem_specs(3), out_specs=vmem_specs(2), name="rows", compiler_params=grant(8),
+    )(fields, near_strip, far_strip)
+    near_rows, far_rows = swapped(near, far, gx[0], counts[0])
     panel = lambda n: pltpu.VMEM((n, tiles + 1, height, LANES), jnp.float32)
     acc_re, acc_im, sums = pl.pallas_call(
-        functools.partial(main_kernel, gx, gy, extents, everyone),
+        functools.partial(main_kernel, gx, gy, everyone),
         out_shape=[shape(rows, cols), shape(rows, cols), shape(everyone, LANES)],
-        in_specs=smem * 3 + vmem_specs(9), out_specs=vmem_specs(3),
+        in_specs=smem + vmem_specs(5), out_specs=vmem_specs(3),
         scratch_shapes=[panel(2), panel(2), panel(2), panel(2), panel(3), panel(2),
                         pltpu.VMEM((TERMS, 8, LANES), jnp.float32),
                         pltpu.VMEM((STEPS * TERMS + STEPS, 8, LANES), jnp.float32)],
-        interpret=interpret, name="chebyshev", compiler_params=grant(20),
-    )(hop_table, centre, duration, *local, from_west, from_east, from_up, from_down)
+        name="chebyshev", compiler_params=grant(20),
+    )(duration, fields, near_strip, far_strip, near_rows, far_rows)
     totals = lax.all_to_all(sums, both, 0, 0, tiled=True)
     out_re, out_im, norms = pl.pallas_call(
         functools.partial(scale_kernel, extents[0] * extents[1]),
         out_shape=[shape(1, rows, cols), shape(1, rows, cols), shape(STEPS, 1, TERMS)],
-        in_specs=vmem_specs(3), out_specs=vmem_specs(3), interpret=interpret, name="scale", compiler_params=grant(4),
+        in_specs=vmem_specs(3), out_specs=vmem_specs(3), name="scale", compiler_params=grant(4),
     )(totals, acc_re, acc_im)
     return out_re, out_im, jnp.swapaxes(norms, 1, 2)
 
 
-def solution(mesh, interpret=False):
+def solution(mesh):
     gx, gy = ("gx",), ("gy",)
     counts = (mesh.shape["gx"], mesh.shape["gy"])
     whole, plane = P(None, "gx", "gy"), P("gx", "gy")
     return jax.shard_map(
-        functools.partial(per_device, gx, gy, counts, interpret),
+        functools.partial(per_device, gx, gy, counts),
         mesh=mesh,
         in_specs=(whole, whole, plane, plane, plane, P(), P(), P()),
         out_specs=(whole, whole, P()),

time: 88.7 us -> 69 us (0.78)
  blocking collectives: 35.1 us -> 46.4 us
  Pallas kernels: 17.8 us -> 7.83 us
  waiting for transfers between devices: 9.04 us -> 0.01 us
  starting transfers between devices: 19.2 us -> 13.2 us
  local copies, waits for them, and re-layouts: 5.85 us -> 0 us
    all_gather x0 -> x2, blocking collectives: none -> 12 us  [swapped(): lax.all_gather(near, axis, axis=0, tiled=True, axis_index_groups=near_pai...]
    pallas_call x3, Pallas kernels: 16.9 us -> 6.95 us  [the longest x1 5.32 us: per_device(): pl.pallas_call(functools.partial(main_kernel, gx, gy, everyone), out_shap...]
    ppermute x4 -> x2, waiting for transfers between devices: 9.04 us -> 0.01 us  [swapped(): from_far = lax.ppermute(far, axis, far_pairs(count))]
    ppermute x4 -> x2, starting transfers between devices: 19.2 us -> 13.2 us  [swapped(): from_far = lax.ppermute(far, axis, far_pairs(count))]
    unnamed x28 -> x0, local copies, waits for them, and re-layouts: 5.85 us -> none
  transfers between devices with their start and end apart: 4 -> 2, of which waited for: 2 -> 0; matrix products, arithmetic and copies ran while one was open for 0% -> 0% of each run, Pallas kernels for 0% -> 0%
where the time goes in v2:
time: 69 us; the launch traced here: 68.7 us
  blocking collectives  46.4 us (67%)
  starting transfers between devices  13.2 us (19%)
  Pallas kernels  7.83 us (11%)
  between operations  1.32 us (2%)
    all_to_all x1, blocking collectives, per_device(): totals = lax.all_to_all(sums, both, 0, 0, tiled=True)  34.3 us
    ppermute x2, starting transfers between devices, swapped(): from_far = lax.ppermute(far, axis, far_pairs(count))  13.2 us
    all_gather x2, blocking collectives, swapped(): lax.all_gather(near, axis, axis=0, tiled=True, axis_index_groups=near_pai...  12 us
    pallas_call x1, Pallas kernels, per_device(): pl.pallas_call(functools.partial(main_kernel, gx, gy, everyone), out_shap...  5.32 us
    pallas_call x1, Pallas kernels, per_device(): pl.pallas_call(functools.partial(fields_kernel, gx, gy, extents), out_sha...  1.52 us
  transfers between devices with their start and end apart: 2, of which 0 were waited for; matrix products, arithmetic and copies ran while one was open for 0% of the time, Pallas kernels for 0%

profile of v2, /device:TPU:1, one launch (start us, length us, event | category | flops | bytes accessed | tf_op | source)
XLA Modules:
  0.0 68.7 jit_solution(5499477969960798051)
XLA Ops:
  0.6 1.5 %fields.1 = (f32[5,32,1024]{2,1,0:T(8,128)S(1)}, f32[32,128]{1,0:T(8,128)S(1)}, f32[32,128]{1,0:T(8,128)S(1)}) custom-call(f32[16]{0:T(128)} %table_hbm.1, s32[1,2]{1,0:T(1,128)} %centre_hbm.1, f32[1,32,1024]{2,1,0:T(8,128)} %re.1, f32[1,32,1024]{2,1,0:T(8,128)} %im.1, f32[32,1024]{1,0:T(8,128)} %onsite.1, s32[32,1024]{1,0:T(8,128)} %down.1, s32[32,1024]{1,0:T(8,128)} %right.1), custom_call_target="tpu_custom_call" | custom-call | tf_op jit(solution)/shard_map/fields/pallas_call | solution.py:408
  2.2 6.8 %collective-permute-start = (f32[32,128]{1,0:T(8,128)S(1)}, f32[32,128]{1,0:T(8,128)S(1)}, u32[]{:S(2)}, u32[]{:S(2)}) collective-permute-start(f32[32,128]{1,0:T(8,128)S(1)} %get-tuple-element.16), channel_id=1, source_target_pairs={{1,2},{3,4},{5,6},{7,8},{9,10},{11,12},{13,14},{15,0},{2,1},{4,3},... | collective-permute-start | bytes 49160 | tf_op jit(solution)/shard_map/ppermute | solution.py:380
  9.0 3.3 %all_gather.6.near_strip = f32[64,128]{1,0:T(8,128)S(1)} all-gather(f32[32,128]{1,0:T(8,128)S(1)} %get-tuple-element.15), channel_id=1, replica_groups={{0,1},{2,3},{4,5},{6,7},{8,9},{10,11},{12,13},{14,15},{16,17},{18,19},{..., dimensions={0}, use_global_device_ids=true | all-gather | bytes 49152 | tf_op jit(solution)/shard_map/all_gather | solution.py:381
  12.3 0.0 collective-permute-done.far_strip
  12.3 0.1 rows.1
  12.4 6.4 %collective-permute-start.1 = (f32[72,1152]{1,0:T(8,128)S(1)}, f32[72,1152]{1,0:T(8,128)S(1)}, u32[]{:S(2)}, u32[]{:S(2)}) collective-permute-start(f32[72,1152]{1,0:T(8,128)S(1)} %get-tuple-element.18), channel_id=1, source_target_pairs={{16,32},{48,64},{80,96},{112,128},{144,160},{176,192},{208,224},{2... | collective-permute-start | bytes 995336 | tf_op jit(solution)/shard_map/ppermute | solution.py:380
  19.4 8.8 %all_gather.7.near_rows = f32[144,1152]{1,0:T(8,128)S(1)} all-gather(f32[72,1152]{1,0:T(8,128)S(1)} %get-tuple-element.17), channel_id=1, replica_groups={{0,16},{32,48},{64,80},{96,112},{128,144},{160,176},{192,208},{224,240}..., dimensions={0}, use_global_device_ids=true | all-gather | bytes 995328 | tf_op jit(solution)/shard_map/all_gather | solution.py:381
  28.2 0.0 collective-permute-done.1.far_rows
  28.2 5.3 %chebyshev.1 = (f32[32,1024]{1,0:T(8,128)S(1)}, f32[32,1024]{1,0:T(8,128)S(1)}, f32[512,128]{1,0:T(8,128)S(1)}) custom-call(f32[1]{0:T(128)S(6)} %copy.14.duration_ref, f32[5,32,1024]{2,1,0:T(8,128)S(1)} %get-tuple-element.14.fields_ref, f32[64,128]{1,0:T(8,128)S(1)} %all_gather.6.near_strip, f32[32,128]{1,0:T(8,128)S(1)} %collective-permute-done.far_strip, ...), custom_call_target="tpu_custom_call" | custom-call | tf_op jit(solution)/shard_map/chebyshev/pallas_call | solution.py:425
  33.5 34.3 %all_to_all.11 = f32[512,1,128]{2,1,0:T(1,128)S(1)} all-to-all(f32[512,1,128]{2,1,0:T(1,128)S(1)} %bitcast.8), channel_id=1, replica_groups=mesh['gx'=32,'gy'=16] {'gx','gy'}, dimensions={0} | all-to-all | bytes 524288 | tf_op jit(solution)/shard_map/all_to_all | solution.py:434
  67.8 0.9 %scale.1 = (f32[1,32,1024]{2,1,0:T(8,128)}, f32[1,32,1024]{2,1,0:T(8,128)}, f32[2,1,8]{2,1,0:T(1,128)}) custom-call(f32[512,128]{1,0:T(8,128)S(1)} %bitcast.7, f32[32,1024]{1,0:T(8,128)S(1)} %get-tuple-element.20.re_ref, f32[32,1024]{1,0:T(8,128)S(1)} %get-tuple-element.21.im_ref), custom_call_target="tpu_custom_call" | custom-call | tf_op jit(solution)/shard_map/scale/pallas_call | solution.py:435
Async XLA Ops:
  2.2 10.1 %collective-permute-start = (f32[32,128]{1,0:T(8,128)S(1)}, f32[32,128]{1,0:T(8,128)S(1)}, u32[]{:S(2)}, u32[]{:S(2)}) collective-permute-start(f32[32,128]{1,0:T(8,128)S(1)} %get-tuple-element.16), channel_id=1, source_target_pairs={{1,2},{3,4},{5,6},{7,8},{9,10},{11,12},{13,14},{15,0},{2,1},{4,3},... | collective-permute-start | bytes 49160 | tf_op jit(solution)/shard_map/ppermute | solution.py:380
  12.4 15.8 %collective-permute-start.1 = (f32[72,1152]{1,0:T(8,128)S(1)}, f32[72,1152]{1,0:T(8,128)S(1)}, u32[]{:S(2)}, u32[]{:S(2)}) collective-permute-start(f32[72,1152]{1,0:T(8,128)S(1)} %get-tuple-element.18), channel_id=1, source_target_pairs={{16,32},{48,64},{80,96},{112,128},{144,160},{176,192},{208,224},{2... | collective-permute-start | bytes 995336 | tf_op jit(solution)/shard_map/ppermute | solution.py:380

commit v3 on v2

--- a/solution.py
+++ b/solution.py
@@ -62,7 +62,7 @@
     return lax.axis_index(gx) * rows, lax.axis_index(gy) * cols
 
 
-def fields_kernel(gx, gy, extents, table_hbm, centre_hbm, re, im, onsite, down, right, fields_ref, near_ref, far_ref,
+def fields_kernel(gx, gy, extents, table_hbm, centre_hbm, re, im, onsite, down, right, fields_ref, near_ref, far_ref, far_rows_ref,
                   table_ref, centre_ref, fine, codes, sems):
     rows, cols = onsite.shape
     copies = [
@@ -113,6 +113,13 @@
     odd = lax.rem(lax.axis_index(gy), 2) == 1
     near_ref[...] = jnp.where(odd, west, east)
     far_ref[...] = jnp.where(odd, east, west)
+    row_parity = lax.rem(lax.axis_index(gx), 2)
+    for parity, first in ((0, 0), (1, rows - REACH)):
+
+        @pl.when(row_parity == parity)
+        def _(first=first):
+            for index in range(FIELDS):
+                far_rows_ref[index * REACH : (index + 1) * REACH, :] = fields_ref[index, first : first + REACH, :]
 
 
 def strips_from(gy, near_ref, far_ref):
@@ -131,27 +138,27 @@
     return jnp.where(lane < REACH, right, jnp.where(lane >= LANES - REACH, left, 0.0))
 
 
-def rows_kernel(gx, gy, fields_ref, near_strip, far_strip, near_ref, far_ref):
+def rows_kernel(gx, gy, fields_ref, near_strip, far_strip, near_ref, corner_ref):
     _, rows, cols = fields_ref.shape
     from_west, from_east = strips_from(gy, near_strip, far_strip)
     parity = lax.rem(lax.axis_index(gx), 2)
 
-    def fill(first, out_ref):
-        west, east = (r[first : first + REACH, :] for r in (from_west, from_east))
+    def fill(near_first, far_first):
         for index in range(FIELDS):
             at = slice(index * REACH, (index + 1) * REACH)
-            out_ref[at, cols : cols + LANES] = halo_columns(west, east, index)
-            out_ref[at, :cols] = fields_ref[index, first : first + REACH, :]
+            cut = slice(near_first, near_first + REACH)
+            near_ref[at, cols : cols + LANES] = halo_columns(from_west[cut], from_east[cut], index)
+            near_ref[at, :cols] = fields_ref[index, cut, :]
+            cut = slice(far_first, far_first + REACH)
+            corner_ref[at, :] = halo_columns(from_west[cut], from_east[cut], index)
 
     @pl.when(parity == 0)
     def _():
-        fill(0, far_ref)
-        fill(rows - REACH, near_ref)
+        fill(rows - REACH, 0)
 
     @pl.when(parity == 1)
     def _():
-        fill(0, near_ref)
-        fill(rows - REACH, far_ref)
+        fill(0, rows - REACH)
 
 
 def bessel_weights(duration):
@@ -170,7 +177,7 @@
 
 
 def main_kernel(gx, gy, copies, duration_ref, fields_ref,
-                near_strip, far_strip, near_rows, far_rows, out_re, out_im, sums_ref,
+                near_strip, far_strip, near_rows, far_rows, far_corner, out_re, out_im, sums_ref,
                 psi, odd, even, total, coeffs, up_left, weight_ref, norm_ref):
     _, rows, cols = fields_ref.shape
     tiles = cols // LANES
@@ -197,7 +204,10 @@
             for index, (target, scale) in enumerate(zip(targets, scales)):
                 first = base + index * REACH
                 for tile in range(tiles + 1):
-                    value = source[first : first + REACH, tile * LANES : (tile + 1) * LANES]
+                    if tile == tiles and source is far_rows:
+                        value = far_corner[first : first + REACH, :]
+                    else:
+                        value = source[first : first + REACH, tile * LANES : (tile + 1) * LANES]
                     target[tile, start : start + REACH, :] = value if scale == 1.0 else value * scale
 
     row_parity = lax.rem(lax.axis_index(gx), 2)
@@ -376,10 +386,12 @@
     return [[i, i + 1] for i in range(0, count, 2)]
 
 
-def swapped(near, far, axis, count):
-    from_far = lax.ppermute(far, axis, far_pairs(count))
-    from_near = lax.all_gather(near, axis, axis=0, tiled=True, axis_index_groups=near_pairs(count))
-    return from_near, from_far
+def from_far_one(value, axis, count):
+    return lax.ppermute(value, axis, far_pairs(count))
+
+
+def from_near_one(value, axis, count):
+    return lax.all_gather(value, axis, axis=0, tiled=True, axis_index_groups=near_pairs(count))
 
 
 FIELDS_PARAMS = pltpu.CompilerParams(vmem_limit_bytes=20 * 2**20)
@@ -405,32 +417,35 @@
     height = rows + 2 * TOP + 2 * PAD
 
     hbm = [pl.BlockSpec(memory_space=pltpu.HBM)]
-    fields, near, far = pl.pallas_call(
+    packed_rows = -(-FIELDS * REACH // 8) * 8
+    fields, near, far, far_main = pl.pallas_call(
         functools.partial(fields_kernel, gx, gy, extents),
-        out_shape=[shape(FIELDS, rows, cols), shape(rows, LANES), shape(rows, LANES)],
-        in_specs=hbm * 7, out_specs=vmem_specs(3),
+        out_shape=[shape(FIELDS, rows, cols), shape(rows, LANES), shape(rows, LANES), shape(packed_rows, cols)],
+        in_specs=hbm * 7, out_specs=vmem_specs(4),
         scratch_shapes=[SMEM(hop_table.shape, jnp.float32), SMEM(centre.shape, jnp.int32), VMEM((2, rows, cols), jnp.float32),
                         VMEM((2, rows, cols), jnp.int32), pltpu.SemaphoreType.DMA((7,))],
         name="fields", compiler_params=FIELDS_PARAMS,
     )(*(pltpu.with_memory_space_constraint(x, pltpu.HBM) for x in (hop_table, centre, *local)))
-    near_strip, far_strip = swapped(near, far, gy[0], counts[1])
-    packed_rows = -(-FIELDS * REACH // 8) * 8
-    near, far = pl.pallas_call(
+    far_rows = from_far_one(far_main, gx[0], counts[0])
+    far_strip = from_far_one(far, gy[0], counts[1])
+    near_strip = from_near_one(near, gy[0], counts[1])
+    near, corner = pl.pallas_call(
         functools.partial(rows_kernel, gx, gy),
-        out_shape=[shape(packed_rows, cols + LANES)] * 2,
+        out_shape=[shape(packed_rows, cols + LANES), shape(packed_rows, LANES)],
         in_specs=vmem_specs(3), out_specs=vmem_specs(2), name="rows", compiler_params=grant(8),
     )(fields, near_strip, far_strip)
-    near_rows, far_rows = swapped(near, far, gx[0], counts[0])
+    far_corner = from_far_one(corner, gx[0], counts[0])
+    near_rows = from_near_one(near, gx[0], counts[0])
     panel = lambda n: pltpu.VMEM((n, tiles + 1, height, LANES), jnp.float32)
     acc_re, acc_im, sums = pl.pallas_call(
         functools.partial(main_kernel, gx, gy, everyone),
         out_shape=[shape(rows, cols), shape(rows, cols), shape(everyone, LANES)],
-        in_specs=smem + vmem_specs(5), out_specs=vmem_specs(3),
+        in_specs=smem + vmem_specs(6), out_specs=vmem_specs(3),
         scratch_shapes=[panel(2), panel(2), panel(2), panel(2), panel(3), panel(2),
                         pltpu.VMEM((TERMS, 8, LANES), jnp.float32),
                         pltpu.VMEM((STEPS * TERMS + STEPS, 8, LANES), jnp.float32)],
         name="chebyshev", compiler_params=grant(20),
-    )(duration, fields, near_strip, far_strip, near_rows, far_rows)
+    )(duration, fields, near_strip, far_strip, near_rows, far_rows, far_corner)
     totals = lax.all_to_all(sums, both, 0, 0, tiled=True)
     out_re, out_im, norms = pl.pallas_call(
         functools.partial(scale_kernel, extents[0] * extents[1]),

time: 69 us -> 68.6 us (level)
  blocking collectives: 46.4 us -> 41.6 us
  starting transfers between devices: 13.2 us -> 17.5 us
    ppermute x2 -> x3, starting transfers between devices: 13.2 us -> 17.5 us  [from_far_one(): return lax.ppermute(value, axis, far_pairs(count))]
    all_to_all x1, blocking collectives: 34.3 us -> 30.8 us  [per_device(): totals = lax.all_to_all(sums, both, 0, 0, tiled=True)]
    all_gather x2, blocking collectives: 12 us -> 10.8 us  [from_near_one(): lax.all_gather(value, axis, axis=0, tiled=True, axis_index_groups=near_pa...]
  transfers between devices with their start and end apart: 2 -> 3, of which waited for: 0 -> 0; matrix products, arithmetic and copies ran while one was open for 0% -> 0% of each run, Pallas kernels for 0% -> 0%
where the time goes in v3:
time: 68.6 us; the launch traced here: 68.3 us
  blocking collectives  41.6 us (61%)
  starting transfers between devices  17.5 us (26%)
  Pallas kernels  7.86 us (11%)
  between operations  1.33 us (2%)
    all_to_all x1, blocking collectives, per_device(): totals = lax.all_to_all(sums, both, 0, 0, tiled=True)  30.8 us
    ppermute x3, starting transfers between devices, from_far_one(): return lax.ppermute(value, axis, far_pairs(count))  17.5 us
    all_gather x2, blocking collectives, from_near_one(): lax.all_gather(value, axis, axis=0, tiled=True, axis_index_groups=near_pa...  10.8 us
    pallas_call x1, Pallas kernels, per_device(): pl.pallas_call(functools.partial(main_kernel, gx, gy, everyone), out_shap...  5.32 us
    pallas_call x1, Pallas kernels, per_device(): pl.pallas_call(functools.partial(fields_kernel, gx, gy, extents), out_sha...  1.55 us
  transfers between devices with their start and end apart: 3, of which 0 were waited for; matrix products, arithmetic and copies ran while one was open for 0% of the time, Pallas kernels for 0%

profile of v3, /device:TPU:1, one launch (start us, length us, event | category | flops | bytes accessed | tf_op | source)
XLA Modules:
  0.0 68.3 jit_solution(1872804182224403099)
XLA Ops:
  0.6 1.6 %fields.1 = (f32[5,32,1024]{2,1,0:T(8,128)S(1)}, f32[32,128]{1,0:T(8,128)S(1)}, f32[32,128]{1,0:T(8,128)S(1)}, f32[72,1024]{1,0:T(8,128)S(1)}) custom-call(f32[16]{0:T(128)} %table_hbm.1, s32[1,2]{1,0:T(1,128)} %centre_hbm.1, f32[1,32,1024]{2,1,0:T(8,128)} %re.1, f32[1,32,1024]{2,1,0:T(8,128)} %im.1, f32[32,1024]{1,0:T(8,128)} %onsite.1, s32[32,1024]{1,0:T(8,128)} %down.1, ...), custom_call_target="tpu_custom_call" | custom-call | tf_op jit(solution)/shard_map/fields/pallas_call | solution.py:421
  2.2 6.0 %collective-permute-start.1 = (f32[72,1024]{1,0:T(8,128)S(1)}, f32[72,1024]{1,0:T(8,128)S(1)}, u32[]{:S(2)}, u32[]{:S(2)}) collective-permute-start(f32[72,1024]{1,0:T(8,128)S(1)} %get-tuple-element.19), channel_id=1, source_target_pairs={{16,32},{48,64},{80,96},{112,128},{144,160},{176,192},{208,224},{2... | collective-permute-start | bytes 884744 | tf_op jit(solution)/shard_map/ppermute | solution.py:390
  8.2 5.1 %collective-permute-start = (f32[32,128]{1,0:T(8,128)S(1)}, f32[32,128]{1,0:T(8,128)S(1)}, u32[]{:S(2)}, u32[]{:S(2)}) collective-permute-start(f32[32,128]{1,0:T(8,128)S(1)} %get-tuple-element.17), channel_id=1, source_target_pairs={{1,2},{3,4},{5,6},{7,8},{9,10},{11,12},{13,14},{15,0},{2,1},{4,3},... | collective-permute-start | bytes 49160 | tf_op jit(solution)/shard_map/ppermute | solution.py:390
  14.0 3.5 %all_gather.6.near_strip = f32[64,128]{1,0:T(8,128)S(1)} all-gather(f32[32,128]{1,0:T(8,128)S(1)} %get-tuple-element.16), channel_id=1, replica_groups={{0,1},{2,3},{4,5},{6,7},{8,9},{10,11},{12,13},{14,15},{16,17},{18,19},{..., dimensions={0}, use_global_device_ids=true | all-gather | bytes 49152 | tf_op jit(solution)/shard_map/all_gather | solution.py:394
  17.5 0.0 collective-permute-done.far_strip
  17.5 0.1 rows.1
  17.7 6.4 %collective-permute-start.2 = (f32[72,128]{1,0:T(8,128)S(1)}, f32[72,128]{1,0:T(8,128)S(1)}, u32[]{:S(2)}, u32[]{:S(2)}) collective-permute-start(f32[72,128]{1,0:T(8,128)S(1)} %get-tuple-element.20), channel_id=1, source_target_pairs={{16,32},{48,64},{80,96},{112,128},{144,160},{176,192},{208,224},{2... | collective-permute-start | bytes 110600 | tf_op jit(solution)/shard_map/ppermute | solution.py:390
  24.0 7.3 %all_gather.7.near_rows = f32[144,1152]{1,0:T(8,128)S(1)} all-gather(f32[72,1152]{1,0:T(8,128)S(1)} %get-tuple-element.18), channel_id=1, replica_groups={{0,16},{32,48},{64,80},{96,112},{128,144},{160,176},{192,208},{224,240}..., dimensions={0}, use_global_device_ids=true | all-gather | bytes 995328 | tf_op jit(solution)/shard_map/all_gather | solution.py:394
  31.3 0.0 collective-permute-done.2.far_corner
  31.3 0.0 collective-permute-done.1.far_rows
  31.3 5.3 %chebyshev.1 = (f32[32,1024]{1,0:T(8,128)S(1)}, f32[32,1024]{1,0:T(8,128)S(1)}, f32[512,128]{1,0:T(8,128)S(1)}) custom-call(f32[1]{0:T(128)S(6)} %copy.14.duration_ref, f32[5,32,1024]{2,1,0:T(8,128)S(1)} %get-tuple-element.15.fields_ref, f32[64,128]{1,0:T(8,128)S(1)} %all_gather.6.near_strip, f32[32,128]{1,0:T(8,128)S(1)} %collective-permute-done.far_strip, ...), custom_call_target="tpu_custom_call" | custom-call | tf_op jit(solution)/shard_map/chebyshev/pallas_call | solution.py:440
  36.7 30.8 %all_to_all.11 = f32[512,1,128]{2,1,0:T(1,128)S(1)} all-to-all(f32[512,1,128]{2,1,0:T(1,128)S(1)} %bitcast.8), channel_id=1, replica_groups=mesh['gx'=32,'gy'=16] {'gx','gy'}, dimensions={0} | all-to-all | bytes 524288 | tf_op jit(solution)/shard_map/all_to_all | solution.py:449
  67.4 0.9 %scale.1 = (f32[1,32,1024]{2,1,0:T(8,128)}, f32[1,32,1024]{2,1,0:T(8,128)}, f32[2,1,8]{2,1,0:T(1,128)}) custom-call(f32[512,128]{1,0:T(8,128)S(1)} %bitcast.7, f32[32,1024]{1,0:T(8,128)S(1)} %get-tuple-element.22.re_ref, f32[32,1024]{1,0:T(8,128)S(1)} %get-tuple-element.23.im_ref), custom_call_target="tpu_custom_call" | custom-call | tf_op jit(solution)/shard_map/scale/pallas_call | solution.py:450
Async XLA Ops:
  2.2 29.1 %collective-permute-start.1 = (f32[72,1024]{1,0:T(8,128)S(1)}, f32[72,1024]{1,0:T(8,128)S(1)}, u32[]{:S(2)}, u32[]{:S(2)}) collective-permute-start(f32[72,1024]{1,0:T(8,128)S(1)} %get-tuple-element.19), channel_id=1, source_target_pairs={{16,32},{48,64},{80,96},{112,128},{144,160},{176,192},{208,224},{2... | collective-permute-start | bytes 884744 | tf_op jit(solution)/shard_map/ppermute | solution.py:390
  8.2 9.3 %collective-permute-start = (f32[32,128]{1,0:T(8,128)S(1)}, f32[32,128]{1,0:T(8,128)S(1)}, u32[]{:S(2)}, u32[]{:S(2)}) collective-permute-start(f32[32,128]{1,0:T(8,128)S(1)} %get-tuple-element.17), channel_id=1, source_target_pairs={{1,2},{3,4},{5,6},{7,8},{9,10},{11,12},{13,14},{15,0},{2,1},{4,3},... | collective-permute-start | bytes 49160 | tf_op jit(solution)/shard_map/ppermute | solution.py:390
  17.7 13.7 %collective-permute-start.2 = (f32[72,128]{1,0:T(8,128)S(1)}, f32[72,128]{1,0:T(8,128)S(1)}, u32[]{:S(2)}, u32[]{:S(2)}) collective-permute-start(f32[72,128]{1,0:T(8,128)S(1)} %get-tuple-element.20), channel_id=1, source_target_pairs={{16,32},{48,64},{80,96},{112,128},{144,160},{176,192},{208,224},{2... | collective-permute-start | bytes 110600 | tf_op jit(solution)/shard_map/ppermute | solution.py:390

commit v4 on v3

--- a/solution.py
+++ b/solution.py
@@ -6,6 +6,7 @@
 from jax import lax
 from jax.experimental import pallas as pl
 from jax.experimental.pallas import tpu as pltpu
+from jax.sharding import Mesh
 from jax.sharding import PartitionSpec as P
 
 TERMS = 8
@@ -409,8 +410,7 @@
     rows, cols = onsite.shape
     extents = (rows * counts[0], cols * counts[1])
     tiles = cols // LANES
-    both = gx + gy
-    everyone = counts[0] * counts[1]
+    chips = counts[0] * counts[1] // 2
     smem = [pl.BlockSpec(memory_space=SMEM)]
     local = (init_re, init_im, onsite, bond_x, bond_y)
     shape = lambda *s: jax.ShapeDtypeStruct(s, jnp.float32)
@@ -426,7 +426,7 @@
                         VMEM((2, rows, cols), jnp.int32), pltpu.SemaphoreType.DMA((7,))],
         name="fields", compiler_params=FIELDS_PARAMS,
     )(*(pltpu.with_memory_space_constraint(x, pltpu.HBM) for x in (hop_table, centre, *local)))
-    far_rows = from_far_one(far_main, gx[0], counts[0])
+    far_rows = from_far_one(far_main, gx, counts[0])
     far_strip = from_far_one(far, gy[0], counts[1])
     near_strip = from_near_one(near, gy[0], counts[1])
     near, corner = pl.pallas_call(
@@ -434,19 +434,21 @@
         out_shape=[shape(packed_rows, cols + LANES), shape(packed_rows, LANES)],
         in_specs=vmem_specs(3), out_specs=vmem_specs(2), name="rows", compiler_params=grant(8),
     )(fields, near_strip, far_strip)
-    far_corner = from_far_one(corner, gx[0], counts[0])
-    near_rows = from_near_one(near, gx[0], counts[0])
+    far_corner = from_far_one(corner, gx, counts[0])
+    near_rows = from_near_one(near, gx, counts[0])
     panel = lambda n: pltpu.VMEM((n, tiles + 1, height, LANES), jnp.float32)
     acc_re, acc_im, sums = pl.pallas_call(
-        functools.partial(main_kernel, gx, gy, everyone),
-        out_shape=[shape(rows, cols), shape(rows, cols), shape(everyone, LANES)],
+        functools.partial(main_kernel, gx, gy, chips),
+        out_shape=[shape(rows, cols), shape(rows, cols), shape(chips, LANES)],
         in_specs=smem + vmem_specs(6), out_specs=vmem_specs(3),
         scratch_shapes=[panel(2), panel(2), panel(2), panel(2), panel(3), panel(2),
                         pltpu.VMEM((TERMS, 8, LANES), jnp.float32),
                         pltpu.VMEM((STEPS * TERMS + STEPS, 8, LANES), jnp.float32)],
         name="chebyshev", compiler_params=grant(20),
     )(duration, fields, near_strip, far_strip, near_rows, far_rows, far_corner)
-    totals = lax.all_to_all(sums, both, 0, 0, tiled=True)
+    sums = lax.all_gather(sums, gx[1], axis=0, tiled=True)
+    sums = sums[:chips] + sums[chips:]
+    totals = lax.all_to_all(sums, (gx[0], *gy), 0, 0, tiled=True)
     out_re, out_im, norms = pl.pallas_call(
         functools.partial(scale_kernel, extents[0] * extents[1]),
         out_shape=[shape(1, rows, cols), shape(1, rows, cols), shape(STEPS, 1, TERMS)],
@@ -456,12 +458,13 @@
 
 
 def solution(mesh):
-    gx, gy = ("gx",), ("gy",)
     counts = (mesh.shape["gx"], mesh.shape["gy"])
-    whole, plane = P(None, "gx", "gy"), P("gx", "gy")
+    finer = Mesh(mesh.devices.reshape(counts[0] // 2, 2, counts[1]), ("chip", "core", "gy"))
+    gx, gy = ("chip", "core"), ("gy",)
+    whole, plane = P(None, gx, "gy"), P(gx, "gy")
     return jax.shard_map(
         functools.partial(per_device, gx, gy, counts),
-        mesh=mesh,
+        mesh=finer,
         in_specs=(whole, whole, plane, plane, plane, P(), P(), P()),
         out_specs=(whole, whole, P()),
         check_vma=False,

time: 68.6 us -> 66 us (0.962)
  blocking collectives: 41.6 us -> 39 us
    all_to_all x1, blocking collectives: 30.8 us -> 21.5 us  [per_device(): totals = lax.all_to_all(sums, (gx[0], *gy), 0, 0, tiled=True)]
    all_gather x0 -> x1, blocking collectives: none -> 6.67 us  [per_device(): sums = lax.all_gather(sums, gx[1], axis=0, tiled=True)]
where the time goes in v4:
time: 66 us; the launch traced here: 65.7 us
  blocking collectives  39 us (59%)
  starting transfers between devices  17.5 us (27%)
  Pallas kernels  7.82 us (12%)
  between operations  1.33 us (2%)
    all_to_all x1, blocking collectives, per_device(): totals = lax.all_to_all(sums, (gx[0], *gy), 0, 0, tiled=True)  21.5 us
    ppermute x3, starting transfers between devices, from_far_one(): return lax.ppermute(value, axis, far_pairs(count))  17.5 us
    all_gather x2, blocking collectives, from_near_one(): lax.all_gather(value, axis, axis=0, tiled=True, axis_index_groups=near_pa...  10.8 us
    all_gather x1, blocking collectives, per_device(): sums = lax.all_gather(sums, gx[1], axis=0, tiled=True)  6.67 us
    pallas_call x1, Pallas kernels, per_device(): pl.pallas_call(functools.partial(main_kernel, gx, gy, chips), out_shape=[...  5.31 us
    pallas_call x1, Pallas kernels, per_device(): pl.pallas_call(functools.partial(fields_kernel, gx, gy, extents), out_sha...  1.55 us
  transfers between devices with their start and end apart: 3, of which 0 were waited for; matrix products, arithmetic and copies ran while one was open for 0% of the time, Pallas kernels for 0%

profile of v4, /device:TPU:1, one launch (start us, length us, event | category | flops | bytes accessed | tf_op | source)
XLA Modules:
  0.0 65.7 jit_solution(5283738767749825997)
XLA Ops:
  0.6 1.5 %fields.1 = (f32[5,32,1024]{2,1,0:T(8,128)S(1)}, f32[32,128]{1,0:T(8,128)S(1)}, f32[32,128]{1,0:T(8,128)S(1)}, f32[72,1024]{1,0:T(8,128)S(1)}) custom-call(f32[16]{0:T(128)} %table_hbm.1, s32[1,2]{1,0:T(1,128)} %centre_hbm.1, f32[1,32,1024]{2,1,0:T(8,128)} %re.1, f32[1,32,1024]{2,1,0:T(8,128)} %im.1, f32[32,1024]{1,0:T(8,128)} %onsite.1, s32[32,1024]{1,0:T(8,128)} %down.1, ...), custom_call_target="tpu_custom_call" | custom-call | tf_op jit(solution)/shard_map/fields/pallas_call | solution.py:421
  2.2 6.0 %collective-permute-start.1 = (f32[72,1024]{1,0:T(8,128)S(1)}, f32[72,1024]{1,0:T(8,128)S(1)}, u32[]{:S(2)}, u32[]{:S(2)}) collective-permute-start(f32[72,1024]{1,0:T(8,128)S(1)} %get-tuple-element.19), channel_id=1, source_target_pairs={{16,32},{48,64},{80,96},{112,128},{144,160},{176,192},{208,224},{2... | collective-permute-start | bytes 884744 | tf_op jit(solution)/shard_map/ppermute | solution.py:391
  8.2 5.1 %collective-permute-start = (f32[32,128]{1,0:T(8,128)S(1)}, f32[32,128]{1,0:T(8,128)S(1)}, u32[]{:S(2)}, u32[]{:S(2)}) collective-permute-start(f32[32,128]{1,0:T(8,128)S(1)} %get-tuple-element.17), channel_id=1, source_target_pairs={{1,2},{3,4},{5,6},{7,8},{9,10},{11,12},{13,14},{15,0},{2,1},{4,3},... | collective-permute-start | bytes 49160 | tf_op jit(solution)/shard_map/ppermute | solution.py:391
  14.0 3.5 %all_gather.9.near_strip = f32[64,128]{1,0:T(8,128)S(1)} all-gather(f32[32,128]{1,0:T(8,128)S(1)} %get-tuple-element.16), channel_id=1, replica_groups={{0,1},{2,3},{4,5},{6,7},{8,9},{10,11},{12,13},{14,15},{16,17},{18,19},{..., dimensions={0}, use_global_device_ids=true | all-gather | bytes 49152 | tf_op jit(solution)/shard_map/all_gather | solution.py:395
  17.5 0.0 collective-permute-done.far_strip
  17.5 0.1 rows.1
  17.7 6.4 %collective-permute-start.2 = (f32[72,128]{1,0:T(8,128)S(1)}, f32[72,128]{1,0:T(8,128)S(1)}, u32[]{:S(2)}, u32[]{:S(2)}) collective-permute-start(f32[72,128]{1,0:T(8,128)S(1)} %get-tuple-element.20), channel_id=1, source_target_pairs={{16,32},{48,64},{80,96},{112,128},{144,160},{176,192},{208,224},{2... | collective-permute-start | bytes 110600 | tf_op jit(solution)/shard_map/ppermute | solution.py:391
  24.0 7.3 %all_gather.10.near_rows = f32[144,1152]{1,0:T(8,128)S(1)} all-gather(f32[72,1152]{1,0:T(8,128)S(1)} %get-tuple-element.18), channel_id=1, replica_groups={{0,16},{32,48},{64,80},{96,112},{128,144},{160,176},{192,208},{224,240}..., dimensions={0}, use_global_device_ids=true | all-gather | bytes 995328 | tf_op jit(solution)/shard_map/all_gather | solution.py:395
  31.3 0.0 collective-permute-done.2.far_corner
  31.3 0.0 collective-permute-done.1.far_rows
  31.3 5.3 %chebyshev.1 = (f32[32,1024]{1,0:T(8,128)S(1)}, f32[32,1024]{1,0:T(8,128)S(1)}, f32[256,128]{1,0:T(8,128)S(1)}) custom-call(f32[1]{0:T(128)S(6)} %copy.14.duration_ref, f32[5,32,1024]{2,1,0:T(8,128)S(1)} %get-tuple-element.15.fields_ref, f32[64,128]{1,0:T(8,128)S(1)} %all_gather.9.near_strip, f32[32,128]{1,0:T(8,128)S(1)} %collective-permute-done.far_strip, ...), custom_call_target="tpu_custom_call" | custom-call | tf_op jit(solution)/shard_map/chebyshev/pallas_call | solution.py:440
  36.6 6.7 %all_gather.11 = f32[512,128]{1,0:T(8,128)S(1)} all-gather(f32[256,128]{1,0:T(8,128)S(1)} %get-tuple-element.21), channel_id=1, replica_groups=mesh['chip'=16,'core'=2,'gy'=16] {'core'}, dimensions={0}, use_global_device_ids=true | all-gather | bytes 393216 | tf_op jit(solution)/shard_map/all_gather | solution.py:449
  43.3 21.5 %all_to_all.11 = f32[256,1,128]{2,1,0:T(1,128)S(1)} all-to-all(f32[256,1,128]{2,1,0:T(1,128)S(1)} %bitcast.8), channel_id=1, replica_groups=mesh['chip'=16,'core'=2,'gy'=16] {'chip','gy'}, dimensions={0} | all-to-all | bytes 262144 | tf_op jit(solution)/shard_map/all_to_all | solution.py:451
  64.8 0.8 %scale.1 = (f32[1,32,1024]{2,1,0:T(8,128)}, f32[1,32,1024]{2,1,0:T(8,128)}, f32[2,1,8]{2,1,0:T(1,128)}) custom-call(f32[256,128]{1,0:T(8,128)S(1)} %bitcast.7, f32[32,1024]{1,0:T(8,128)S(1)} %get-tuple-element.22.re_ref, f32[32,1024]{1,0:T(8,128)S(1)} %get-tuple-element.23.im_ref), custom_call_target="tpu_custom_call" | custom-call | tf_op jit(solution)/shard_map/scale/pallas_call | solution.py:452
  (1 shorter events, 0.0 us)
Async XLA Ops:
  2.2 29.1 %collective-permute-start.1 = (f32[72,1024]{1,0:T(8,128)S(1)}, f32[72,1024]{1,0:T(8,128)S(1)}, u32[]{:S(2)}, u32[]{:S(2)}) collective-permute-start(f32[72,1024]{1,0:T(8,128)S(1)} %get-tuple-element.19), channel_id=1, source_target_pairs={{16,32},{48,64},{80,96},{112,128},{144,160},{176,192},{208,224},{2... | collective-permute-start | bytes 884744 | tf_op jit(solution)/shard_map/ppermute | solution.py:391
  8.2 9.3 %collective-permute-start = (f32[32,128]{1,0:T(8,128)S(1)}, f32[32,128]{1,0:T(8,128)S(1)}, u32[]{:S(2)}, u32[]{:S(2)}) collective-permute-start(f32[32,128]{1,0:T(8,128)S(1)} %get-tuple-element.17), channel_id=1, source_target_pairs={{1,2},{3,4},{5,6},{7,8},{9,10},{11,12},{13,14},{15,0},{2,1},{4,3},... | collective-permute-start | bytes 49160 | tf_op jit(solution)/shard_map/ppermute | solution.py:391
  17.7 13.7 %collective-permute-start.2 = (f32[72,128]{1,0:T(8,128)S(1)}, f32[72,128]{1,0:T(8,128)S(1)}, u32[]{:S(2)}, u32[]{:S(2)}) collective-permute-start(f32[72,128]{1,0:T(8,128)S(1)} %get-tuple-element.20), channel_id=1, source_target_pairs={{16,32},{48,64},{80,96},{112,128},{144,160},{176,192},{208,224},{2... | collective-permute-start | bytes 110600 | tf_op jit(solution)/shard_map/ppermute | solution.py:391

commit v5 on v4

--- a/solution.py
+++ b/solution.py
@@ -245,7 +245,8 @@
             up_left[1, tile, at, :] = pltpu.roll(joined, 1, 1)
         return carry
 
-    lax.fori_loop(0, tiles + 1, shift_coeffs, 0)
+    for tile in range(tiles + 1):
+        shift_coeffs(tile, 0)
 
     def apply(step, degree, current, previous, target):
         level = step * (TERMS - 1) + degree

time: 66 us -> 65.4 us (level)
  no operation moved by 1% of the time
where the time goes in v5:
time: 65.4 us; the launch traced here: 65.1 us
  blocking collectives  39 us (60%)
  starting transfers between devices  17.5 us (27%)
  Pallas kernels  7.23 us (11%)
  between operations  1.33 us (2%)
    all_to_all x1, blocking collectives, per_device(): totals = lax.all_to_all(sums, (gx[0], *gy), 0, 0, tiled=True)  21.5 us
    ppermute x3, starting transfers between devices, from_far_one(): return lax.ppermute(value, axis, far_pairs(count))  17.5 us
    all_gather x2, blocking collectives, from_near_one(): lax.all_gather(value, axis, axis=0, tiled=True, axis_index_groups=near_pa...  10.8 us
    all_gather x1, blocking collectives, per_device(): sums = lax.all_gather(sums, gx[1], axis=0, tiled=True)  6.67 us
    pallas_call x1, Pallas kernels, per_device(): pl.pallas_call(functools.partial(main_kernel, gx, gy, chips), out_shape=[...  4.73 us
    pallas_call x1, Pallas kernels, per_device(): pl.pallas_call(functools.partial(fields_kernel, gx, gy, extents), out_sha...  1.55 us
  transfers between devices with their start and end apart: 3, of which 0 were waited for; matrix products, arithmetic and copies ran while one was open for 0% of the time, Pallas kernels for 0%

profile of v5, /device:TPU:1, one launch (start us, length us, event | category | flops | bytes accessed | tf_op | source)
XLA Modules:
  0.0 65.1 jit_solution(12104207144993625401)
XLA Ops:
  0.6 1.5 %fields.1 = (f32[5,32,1024]{2,1,0:T(8,128)S(1)}, f32[32,128]{1,0:T(8,128)S(1)}, f32[32,128]{1,0:T(8,128)S(1)}, f32[72,1024]{1,0:T(8,128)S(1)}) custom-call(f32[16]{0:T(128)} %table_hbm.1, s32[1,2]{1,0:T(1,128)} %centre_hbm.1, f32[1,32,1024]{2,1,0:T(8,128)} %re.1, f32[1,32,1024]{2,1,0:T(8,128)} %im.1, f32[32,1024]{1,0:T(8,128)} %onsite.1, s32[32,1024]{1,0:T(8,128)} %down.1, ...), custom_call_target="tpu_custom_call" | custom-call | tf_op jit(solution)/shard_map/fields/pallas_call | solution.py:422
  2.2 6.0 %collective-permute-start.1 = (f32[72,1024]{1,0:T(8,128)S(1)}, f32[72,1024]{1,0:T(8,128)S(1)}, u32[]{:S(2)}, u32[]{:S(2)}) collective-permute-start(f32[72,1024]{1,0:T(8,128)S(1)} %get-tuple-element.19), channel_id=1, source_target_pairs={{16,32},{48,64},{80,96},{112,128},{144,160},{176,192},{208,224},{2... | collective-permute-start | bytes 884744 | tf_op jit(solution)/shard_map/ppermute | solution.py:392
  8.2 5.1 %collective-permute-start = (f32[32,128]{1,0:T(8,128)S(1)}, f32[32,128]{1,0:T(8,128)S(1)}, u32[]{:S(2)}, u32[]{:S(2)}) collective-permute-start(f32[32,128]{1,0:T(8,128)S(1)} %get-tuple-element.17), channel_id=1, source_target_pairs={{1,2},{3,4},{5,6},{7,8},{9,10},{11,12},{13,14},{15,0},{2,1},{4,3},... | collective-permute-start | bytes 49160 | tf_op jit(solution)/shard_map/ppermute | solution.py:392
  14.0 3.5 %all_gather.9.near_strip = f32[64,128]{1,0:T(8,128)S(1)} all-gather(f32[32,128]{1,0:T(8,128)S(1)} %get-tuple-element.16), channel_id=1, replica_groups={{0,1},{2,3},{4,5},{6,7},{8,9},{10,11},{12,13},{14,15},{16,17},{18,19},{..., dimensions={0}, use_global_device_ids=true | all-gather | bytes 49152 | tf_op jit(solution)/shard_map/all_gather | solution.py:396
  17.5 0.0 collective-permute-done.far_strip
  17.5 0.1 rows.1
  17.7 6.4 %collective-permute-start.2 = (f32[72,128]{1,0:T(8,128)S(1)}, f32[72,128]{1,0:T(8,128)S(1)}, u32[]{:S(2)}, u32[]{:S(2)}) collective-permute-start(f32[72,128]{1,0:T(8,128)S(1)} %get-tuple-element.20), channel_id=1, source_target_pairs={{16,32},{48,64},{80,96},{112,128},{144,160},{176,192},{208,224},{2... | collective-permute-start | bytes 110600 | tf_op jit(solution)/shard_map/ppermute | solution.py:392
  24.0 7.3 %all_gather.10.near_rows = f32[144,1152]{1,0:T(8,128)S(1)} all-gather(f32[72,1152]{1,0:T(8,128)S(1)} %get-tuple-element.18), channel_id=1, replica_groups={{0,16},{32,48},{64,80},{96,112},{128,144},{160,176},{192,208},{224,240}..., dimensions={0}, use_global_device_ids=true | all-gather | bytes 995328 | tf_op jit(solution)/shard_map/all_gather | solution.py:396
  31.3 0.0 collective-permute-done.2.far_corner
  31.3 0.0 collective-permute-done.1.far_rows
  31.3 4.7 %chebyshev.1 = (f32[32,1024]{1,0:T(8,128)S(1)}, f32[32,1024]{1,0:T(8,128)S(1)}, f32[256,128]{1,0:T(8,128)S(1)}) custom-call(f32[1]{0:T(128)S(6)} %copy.14.duration_ref, f32[5,32,1024]{2,1,0:T(8,128)S(1)} %get-tuple-element.15.fields_ref, f32[64,128]{1,0:T(8,128)S(1)} %all_gather.9.near_strip, f32[32,128]{1,0:T(8,128)S(1)} %collective-permute-done.far_strip, ...), custom_call_target="tpu_custom_call" | custom-call | tf_op jit(solution)/shard_map/chebyshev/pallas_call | solution.py:441
  36.1 6.7 %all_gather.11 = f32[512,128]{1,0:T(8,128)S(1)} all-gather(f32[256,128]{1,0:T(8,128)S(1)} %get-tuple-element.21), channel_id=1, replica_groups=mesh['chip'=16,'core'=2,'gy'=16] {'core'}, dimensions={0}, use_global_device_ids=true | all-gather | bytes 393216 | tf_op jit(solution)/shard_map/all_gather | solution.py:450
  42.8 21.5 %all_to_all.11 = f32[256,1,128]{2,1,0:T(1,128)S(1)} all-to-all(f32[256,1,128]{2,1,0:T(1,128)S(1)} %bitcast.8), channel_id=1, replica_groups=mesh['chip'=16,'core'=2,'gy'=16] {'chip','gy'}, dimensions={0} | all-to-all | bytes 262144 | tf_op jit(solution)/shard_map/all_to_all | solution.py:452
  64.2 0.8 %scale.1 = (f32[1,32,1024]{2,1,0:T(8,128)}, f32[1,32,1024]{2,1,0:T(8,128)}, f32[2,1,8]{2,1,0:T(1,128)}) custom-call(f32[256,128]{1,0:T(8,128)S(1)} %bitcast.7, f32[32,1024]{1,0:T(8,128)S(1)} %get-tuple-element.22.re_ref, f32[32,1024]{1,0:T(8,128)S(1)} %get-tuple-element.23.im_ref), custom_call_target="tpu_custom_call" | custom-call | tf_op jit(solution)/shard_map/scale/pallas_call | solution.py:453
  (1 shorter events, 0.0 us)
Async XLA Ops:
  2.2 29.1 %collective-permute-start.1 = (f32[72,1024]{1,0:T(8,128)S(1)}, f32[72,1024]{1,0:T(8,128)S(1)}, u32[]{:S(2)}, u32[]{:S(2)}) collective-permute-start(f32[72,1024]{1,0:T(8,128)S(1)} %get-tuple-element.19), channel_id=1, source_target_pairs={{16,32},{48,64},{80,96},{112,128},{144,160},{176,192},{208,224},{2... | collective-permute-start | bytes 884744 | tf_op jit(solution)/shard_map/ppermute | solution.py:392
  8.2 9.3 %collective-permute-start = (f32[32,128]{1,0:T(8,128)S(1)}, f32[32,128]{1,0:T(8,128)S(1)}, u32[]{:S(2)}, u32[]{:S(2)}) collective-permute-start(f32[32,128]{1,0:T(8,128)S(1)} %get-tuple-element.17), channel_id=1, source_target_pairs={{1,2},{3,4},{5,6},{7,8},{9,10},{11,12},{13,14},{15,0},{2,1},{4,3},... | collective-permute-start | bytes 49160 | tf_op jit(solution)/shard_map/ppermute | solution.py:392
  17.7 13.7 %collective-permute-start.2 = (f32[72,128]{1,0:T(8,128)S(1)}, f32[72,128]{1,0:T(8,128)S(1)}, u32[]{:S(2)}, u32[]{:S(2)}) collective-permute-start(f32[72,128]{1,0:T(8,128)S(1)} %get-tuple-element.20), channel_id=1, source_target_pairs={{16,32},{48,64},{80,96},{112,128},{144,160},{176,192},{208,224},{2... | collective-permute-start | bytes 110600 | tf_op jit(solution)/shard_map/ppermute | solution.py:392
